TPU v7x, 32 devices: a whole 2x2x4 slice. The times are simulated.
32 devices in a mesh: grp: 4 (over z), loc: 8 (over y, x, core).
Axes of the slice: x: 2, y: 2, z: 4, core: 2. Of those that a mesh axis runs over, the one named last changes fastest.
Arguments:
- features: float32 [32768, 256], P(('grp', 'loc')), may hold values from -6 to 6
- hub_block: bfloat16 [128, 32768], P(None, ('grp', 'loc')), may hold values from -0.0625 to 0.0625
- hub_slot: int32 [128], P(('grp', 'loc')), may hold values from 0 to 1023, as said below
- neighbours: int32 [32768, 16], P(('grp', 'loc')), may hold values from 0 to 2047
- counts: int32 [32768], P(('grp', 'loc')), may hold values from 1 to 16
- halo_send: int32 [256, 128], P(('grp', 'loc')), may hold values from 0 to 1023
- weight: float32 [256, 256], replicated, may hold values from -0.375 to 0.375
- bias: float32 [256], replicated, may hold values from -3 to 3
Outputs:
- layer_out: float32 [32768, 256], P(('grp', 'loc'))
Inputs may be any that keep to these rules, and one draw needn't show every extreme that they name: `hub_slot`: within each aligned block of 4 entries the values are distinct.
All inputs are finite; a program needn't handle non-finite values.
Results may differ from a plain program's by a relative error of at most 0.0003.
Values sent between devices are 32-bit elements; how exact they have to be, the bound alone decides.
No kernel may reach another device: no remote copies, remote signals or barrier semaphores. Data moves between devices by JAX's collectives and lax.ppermute only.
A program may use at most 64 MiB of HBM per device.

v0:
```python
import functools

import jax
import jax.numpy as jnp
from jax import lax
from jax.experimental import pallas as pl
from jax.experimental.pallas import tpu as pltpu
from jax.sharding import PartitionSpec as P


BF = jnp.bfloat16
F32 = jnp.float32
LANES = 128
STEPS = 4
GROUP = 16


def FLOW(peers):
    return sorted(range(1, peers), key=lambda s: (s < 2, s & 1, -s)) + [0]


def split(x):
    hi = x.astype(BF)
    return hi, (x - hi.astype(F32)).astype(BF)


def mm(a, b, dims=((1,), (0,))):
    return lax.dot_general(a, b, (dims, ((), ())), preferred_element_type=F32)


def pick_kernel(me, features, halo, *refs, peers, rows):
    outs, order = refs[:peers], refs[peers]
    hi, lo = split(features[...])
    own = features.shape[0]
    for s in range(peers):
        order[s : s + 1, :] = halo[pl.ds(me[1] ^ s, 1), :]
    listed = order[...].T
    col = lax.broadcasted_iota(jnp.int32, (rows, own), 1)
    for s in FLOW(peers):
        hot = (listed[:, s : s + 1] == col).astype(F32).astype(BF)
        outs[s][...] = mm(hot, hi) + mm(hot, lo)


def hub_kernel(me, features, hub, *refs, parts):
    outs, full = refs[:parts], refs[parts]
    full[...] = mm(hub[...], features[...].astype(BF))
    size = full.shape[0] // parts
    for s in range(parts):
        at = pl.multiple_of((me[0] ^ s) * size, size)
        outs[s][...] = full[pl.ds(at, size), :]


def inverse_counts(counts):
    return 1.0 / counts[...].astype(F32).T


def count_kernel(features, mine, slots, counts, adj, base, local, *, degree, pool):
    own, _ = features.shape
    rows = mine.shape[0]
    span = GROUP * degree
    near = (own + rows) // LANES
    codes = pool // LANES
    row = lax.broadcasted_iota(jnp.int32, (codes * GROUP, span), 0)
    lane = lax.broadcasted_iota(jnp.int32, (LANES, span), 0)
    vert = lax.broadcasted_iota(jnp.int32, (1, span), 1) // degree

    def build(b, _):
        name = slots[pl.ds(b, 1), :]
        code = jnp.where(name < 0, -1, (name // LANES) * GROUP + vert)
        left = (row == code).astype(F32).astype(BF)
        right = (lane == (name & (LANES - 1))).astype(F32).astype(BF)
        made = mm(left, right, ((1,), (1,))).astype(BF)
        at = pl.multiple_of(b * GROUP, GROUP)
        for h in range(codes):
            part = made[h * GROUP : (h + 1) * GROUP]
            if h < near:
                local[pl.ds(at, GROUP), h * LANES : (h + 1) * LANES] = part
            else:
                adj[pl.ds(at, GROUP), (h - near) * LANES : (h - near + 1) * LANES] = part
        return 0

    lax.fori_loop(0, own // GROUP, build, 0, unroll=4)
    hi, lo = split(jnp.concatenate([features[...], mine[...]], axis=0))
    inv = inverse_counts(counts)
    for j in range(own // LANES):
        cut = slice(j * LANES, (j + 1) * LANES)
        a = local[cut, :]
        base[cut, :] = features[cut, :] + (mm(a, hi) + mm(a, lo)) * inv[:, j : j + 1]


def last_kernel(slot, adj, base, counts, hub, weight, bias, *refs):
    pieces, (out, rhi, rlo, whi, wlo) = refs[:-5], refs[-5:]
    rows, size = base.shape[0], pieces[0].shape[0]
    step = pl.program_id(0)

    @pl.when(step == 0)
    def _():
        for n, piece in enumerate(pieces):
            cut = slice(n * size, (n + 1) * size)
            rhi[cut, :], rlo[cut, :] = split(piece[...])
        whi[...], wlo[...] = split(weight[...])

    inv = inverse_counts(counts)
    a = adj[...]
    summed = mm(a, rhi[...]) + mm(a, rlo[...])
    comb = base[...] + jnp.concatenate(
        [
            summed[j * LANES : (j + 1) * LANES] * inv[:, j : j + 1]
            for j in range(rows // LANES)
        ],
        axis=0,
    )
    row = lax.broadcasted_iota(jnp.int32, (rows, 1), 0) + step * rows
    sums = jnp.sum(hub[...], axis=0)
    for i in range(sums.shape[0]):
        comb = comb + jnp.where(row == slot[i], sums[i : i + 1], 0.0)
    chi, clo = split(comb)
    made = mm(chi, whi[...]) + (mm(chi, wlo[...]) + mm(clo, whi[...])) + bias[...]
    out[...] = jnp.maximum(made, 0.0)


VMEM = pl.BlockSpec(memory_space=pltpu.VMEM)
SMEM = pl.BlockSpec(memory_space=pltpu.SMEM)
PARAMS = pltpu.CompilerParams(vmem_limit_bytes=24 * 1024 * 1024)


def flops(n):
    return pl.CostEstimate(flops=n, bytes_accessed=1 << 20, transcendentals=0)


def on_device(features, hub_block, hub_slot, neighbours, counts, halo_send, weight, bias):
    own, width = features.shape
    degree = neighbours.shape[1]
    n_grp, n_loc = lax.axis_size("grp"), lax.axis_size("loc")
    listed = halo_send.shape[1]
    hubs = hub_block.shape[0]
    owned = hub_slot.shape[0]
    pool = own + n_loc * listed
    here = lax.axis_index("loc").astype(jnp.int32)
    me = jnp.stack([lax.axis_index("grp").astype(jnp.int32), here])

    outgoing = pl.pallas_call(
        functools.partial(pick_kernel, peers=n_loc, rows=listed),
        out_shape=[jax.ShapeDtypeStruct((listed, width), F32)] * n_loc,
        in_specs=[SMEM] + [VMEM] * 2,
        out_specs=[VMEM] * n_loc,
        scratch_shapes=[pltpu.VMEM((n_loc, listed), jnp.int32)],
        compiler_params=PARAMS,
        cost_estimate=flops(4 * n_loc * listed * own * width),
        name="pick",
    )(me, features, halo_send)
    received = []
    for s in range(1, n_loc):
        pairs = [(i, i ^ s) for i in range(n_loc)]
        received.append(lax.ppermute(outgoing[s], "loc", pairs))

    part_rows = hubs // n_grp
    parts = pl.pallas_call(
        functools.partial(hub_kernel, parts=n_grp),
        out_shape=[jax.ShapeDtypeStruct((part_rows, width), F32)] * n_grp,
        in_specs=[SMEM, VMEM, VMEM],
        out_specs=[VMEM] * n_grp,
        scratch_shapes=[pltpu.VMEM((hubs, width), F32)],
        compiler_params=PARAMS,
        cost_estimate=flops(2 * hubs * own * width),
        name="hub",
    )(me, features, hub_block)
    group_part = parts[0]
    for s in range(1, n_grp):
        pairs = [(i, i ^ s) for i in range(n_grp)]
        arrived = lax.ppermute(parts[s], "grp", pairs)
        group_part = group_part + arrived
    group_part = group_part.reshape(n_loc, owned, width)
    hub_pieces = lax.all_to_all(group_part, "loc", split_axis=0, concat_axis=0, tiled=True)

    used = jnp.arange(degree, dtype=jnp.int32)[None, :] < counts[:, None]
    far = neighbours - own
    moved = own + ((far // listed) ^ here) * listed + far % listed
    slots = jnp.where(neighbours < own, neighbours, moved)
    slots = jnp.where(used, slots, -1).reshape(own // GROUP, GROUP * degree)
    counts_rows = counts.reshape(own // LANES, LANES)
    adj, base = pl.pallas_call(
        functools.partial(count_kernel, degree=degree, pool=pool),
        out_shape=[
            jax.ShapeDtypeStruct((own, pool - own - listed), BF),
            jax.ShapeDtypeStruct((own, width), F32),
        ],
        in_specs=[VMEM] * 4,
        out_specs=[VMEM] * 2,
        scratch_shapes=[pltpu.VMEM((own, own + listed), BF)],
        compiler_params=PARAMS,
        cost_estimate=flops(8 * own * own * width),
        name="count",
    )(features, outgoing[0], slots, counts_rows)

    remote = pool - own - listed
    rows = own // STEPS
    whole = lambda *shape: pl.BlockSpec(shape, lambda i: (0,) * len(shape))
    return pl.pallas_call(
        last_kernel,
        out_shape=jax.ShapeDtypeStruct((own, width), F32),
        grid=(STEPS,),
        in_specs=[
            SMEM,
            pl.BlockSpec((rows, remote), lambda i: (i, 0)),
            pl.BlockSpec((rows, width), lambda i: (i, 0)),
            pl.BlockSpec((None, rows // LANES, LANES), lambda i: (i, 0, 0)),
            whole(n_loc, owned, width),
            whole(width, width),
            whole(1, width),
        ]
        + [whole(listed, width)] * (n_loc - 1),
        out_specs=pl.BlockSpec((rows, width), lambda i: (i, 0)),
        scratch_shapes=[pltpu.VMEM((remote, width), BF)] * 2
        + [pltpu.VMEM((width, width), BF)] * 2,
        compiler_params=PARAMS,
        cost_estimate=flops(8 * own * own * width),
        name="last",
    )(
        hub_slot,
        adj,
        base,
        counts.reshape(STEPS, rows // LANES, LANES),
        hub_pieces,
        weight,
        bias.reshape(1, width),
        *received,
    )


def solution(mesh):
    in_specs = (
        P(("grp", "loc"), None),
        P(None, ("grp", "loc")),
        P(("grp", "loc")),
        P(("grp", "loc"), None),
        P(("grp", "loc")),
        P(("grp", "loc"), None),
        P(),
        P(),
    )
    out_specs = P(("grp", "loc"), None)
    return jax.shard_map(
        on_device, mesh=mesh, in_specs=in_specs, out_specs=out_specs, check_vma=False
    )
```

profile of v0, /device:TPU:0, one launch (start us, length us, event | category | flops | bytes accessed | tf_op | source)
XLA Modules:
  0.0 40.2 jit_solution(16912758676946360480)
XLA Ops:
  0.0 0.1 pad_add_fusion.me
  0.1 1.2 %copy-done = f32[1024,256]{1,0:T(8,128)S(1)} copy-done((f32[1024,256]{1,0:T(8,128)S(1)}, f32[1024,256]{1,0:T(8,128)}, u32[]{:S(2)}) %copy-start) | copy-done | bytes 1048600
  1.3 0.9 %copy-done.2 = bf16[128,1024]{1,0:T(8,128)(2,1)S(1)} copy-done((bf16[128,1024]{1,0:T(8,128)(2,1)S(1)}, bf16[128,1024]{1,0:T(8,128)(2,1)}, u32[]{:S(2)}) %copy-start.2) | copy-done | bytes 262168
  2.3 0.8 %hub.2 = (f32[32,256]{1,0:T(8,128)S(1)}, f32[32,256]{1,0:T(8,128)S(1)}, f32[32,256]{1,0:T(8,128)S(1)}, f32[32,256]{1,0:T(8,128)S(1)}) custom-call(s32[2]{0:T(128)S(1)} %pad_add_fusion.me, f32[1024,256]{1,0:T(8,128)S(1)} %copy-done, bf16[128,1024]{1,0:T(8,128)(2,1)S(1)} %copy-done.2), custom_call_target="tpu_custom_call" | custom-call | flops 67108864 | bytes 1048576 | tf_op jit(solution)/shard_map/hub/pallas_call | solution.py:158
  3.1 3.1 %collective-permute-start = (f32[32,256]{1,0:T(8,128)S(1)}, f32[32,256]{1,0:T(8,128)S(1)}, u32[]{:S(2)}, u32[]{:S(2)}) collective-permute-start(f32[32,256]{1,0:T(8,128)S(1)} %get-tuple-element.23), channel_id=1, source_target_pairs={{0,8},{8,0},{16,24},{24,16},{1,9},{9,1},{17,25},{25,17},{2,10},{10... | collective-permute-start | bytes 98312 | tf_op jit(solution)/shard_map/ppermute | solution.py:171
  6.2 2.6 %collective-permute-start.1 = (f32[32,256]{1,0:T(8,128)S(1)}, f32[32,256]{1,0:T(8,128)S(1)}, u32[]{:S(2)}, u32[]{:S(2)}) collective-permute-start(f32[32,256]{1,0:T(8,128)S(1)} %get-tuple-element.24), channel_id=1, source_target_pairs={{0,16},{8,24},{16,0},{24,8},{1,17},{9,25},{17,1},{25,9},{2,18},{10... | collective-permute-start | bytes 98312 | tf_op jit(solution)/shard_map/ppermute | solution.py:171
  8.8 0.0 collective-permute-start.2
  8.8 0.8 %copy-done.5 = s32[8,128]{1,0:T(8,128)S(1)} copy-done((s32[8,128]{1,0:T(8,128)S(1)}, s32[8,128]{1,0:T(8,128)}, u32[]{:S(2)}) %copy-start.5) | copy-done | bytes 4120
  9.6 2.0 %pick.1 = (f32[128,256]{1,0:T(8,128)S(1)}, f32[128,256]{1,0:T(8,128)S(1)}, f32[128,256]{1,0:T(8,128)S(1)}, f32[128,256]{1,0:T(8,128)S(1)}, f32[128,256]{1,0:T(8,...) custom-call(s32[2]{0:T(128)S(1)} %pad_add_fusion.me, f32[1024,256]{1,0:T(8,128)S(1)} %copy-done, ...), custom_call_target="tpu_custom_call" | custom-call | flops 1073741824 | bytes 1048576 | tf_op jit(solution)/shard_map/pick/pallas_call | solution.py:142
  11.6 0.1 collective-permute-start.3
  11.7 1.8 %collective-permute-start.4 = (f32[128,256]{1,0:T(8,128)S(1)}, f32[128,256]{1,0:T(8,128)S(1)}, u32[]{:S(2)}, u32[]{:S(2)}) collective-permute-start(f32[128,256]{1,0:T(8,128)S(1)} %get-tuple-element.27), channel_id=1, source_target_pairs={{0,2},{1,3},{2,0},{3,1},{4,6},{5,7},{6,4},{7,5},{8,10},{9,11},{10,... | collective-permute-start | bytes 393224 | tf_op jit(solution)/shard_map/ppermute | solution.py:155
  13.5 0.1 fusion.4
  13.5 0.2 copy.10
  13.7 0.2 reshape.16.slots
  14.0 0.1 collective-permute-start.5
  14.1 0.0 collective-permute-done.1
  14.1 1.8 %collective-permute-start.6 = (f32[128,256]{1,0:T(8,128)S(1)}, f32[128,256]{1,0:T(8,128)S(1)}, u32[]{:S(2)}, u32[]{:S(2)}) collective-permute-start(f32[128,256]{1,0:T(8,128)S(1)} %get-tuple-element.29), channel_id=1, source_target_pairs={{0,4},{1,5},{2,6},{3,7},{4,0},{5,1},{6,2},{7,3},{8,12},{9,13},{10,... | collective-permute-start | bytes 393224 | tf_op jit(solution)/shard_map/ppermute | solution.py:155
  15.9 0.0 collective-permute-start.7
  15.9 0.6 %reshape.19 = f32[8,4,256]{2,1,0:T(4,128)} reshape(f32[32,256]{1,0:T(8,128)S(1)} %add_add_fusion) | data formatting | bytes 65536 | tf_op jit(solution)/shard_map/reshape | solution.py:173
  16.5 3.9 %all-to-all-start = ((f32[8,4,256]{2,1,0:T(4,128)}), f32[8,4,256]{2,1,0:T(4,128)S(1)}, u32[]{:S(2)}, u32[]{:S(2)}) async-start(f32[8,4,256]{2,1,0:T(4,128)} %reshape.19), calls=%async_computation | async-start | bytes 65536 | tf_op jit(solution)/shard_map/all_to_all | solution.py:174
  20.5 2.9 %collective-permute-start.8 = (f32[128,256]{1,0:T(8,128)S(1)}, f32[128,256]{1,0:T(8,128)S(1)}, u32[]{:S(2)}, u32[]{:S(2)}) collective-permute-start(f32[128,256]{1,0:T(8,128)S(1)} %get-tuple-element.31), channel_id=1, source_target_pairs={{0,6},{1,7},{2,4},{3,5},{4,2},{5,3},{6,0},{7,1},{8,14},{9,15},{10,... | collective-permute-start | bytes 393224 | tf_op jit(solution)/shard_map/ppermute | solution.py:155
  23.4 0.0 copy-start.4
  23.4 0.0 copy-start.6
  23.4 0.0 copy-start.7
  23.4 6.6 %count.1 = (bf16[1024,896]{1,0:T(8,128)(2,1)S(1)}, f32[1024,256]{1,0:T(8,128)S(1)}) custom-call(f32[1024,256]{1,0:T(8,128)S(1)} %copy-done.1, f32[128,256]{1,0:T(8,128)S(1)} %get-tuple-element.19.mine, s32[64,256]{1,0:T(8,128)S(1)} %reshape.16.slots, s32[8,128]{1,0:T(8,128)S(1)} %bitcast.5), custom_call_target="tpu_custom_call" | custom-call | flops 2147483648 | bytes 1048576 | tf_op jit(solution)/shard_map/count/pallas_call | solution.py:182
  30.1 1.2 %copy-done.8 = bf16[1024,896]{1,0:T(8,128)(2,1)} copy-done((bf16[1024,896]{1,0:T(8,128)(2,1)}, bf16[1024,896]{1,0:T(8,128)(2,1)S(1)}, u32[]{:S(2)}) %copy-start.8) | copy-done | bytes 1835032
  31.3 1.0 %copy-done.10 = f32[1024,256]{1,0:T(8,128)} copy-done((f32[1024,256]{1,0:T(8,128)}, f32[1024,256]{1,0:T(8,128)S(1)}, u32[]{:S(2)}) %copy-start.10) | copy-done | bytes 1048600
  32.3 0.0 all-to-all-done.hub
  32.3 0.0 collective-permute-done.5.refs_2_
  32.4 1.5 %copy-done.9 = bf16[1024,896]{1,0:T(8,128)(2,1)S(1)} copy-done((bf16[1024,896]{1,0:T(8,128)(2,1)S(1)}, bf16[1024,896]{1,0:T(8,128)(2,1)}, u32[]{:S(2)}) %copy-start.9) | copy-done | bytes 1835032
  33.9 1.2 %copy-done.11 = f32[1024,256]{1,0:T(8,128)S(1)} copy-done((f32[1024,256]{1,0:T(8,128)S(1)}, f32[1024,256]{1,0:T(8,128)}, u32[]{:S(2)}) %copy-start.11) | copy-done | bytes 1048600
  35.1 5.1 %last.1 = f32[1024,256]{1,0:T(8,128)} custom-call(s32[4]{0:T(128)S(1)} %copy-done.7, bf16[1024,896]{1,0:T(8,128)(2,1)S(1)} %copy-done.9, f32[1024,256]{1,0:T(8,128)S(1)} %copy-done.11, s32[4,2,128]{2,1,0:T(2,128)S(1)} %bitcast.6, f32[8,4,256]{2,1,0:T(4,128)S(1)} %all-to-all-done.hub, f32[256,256]{1,0:T(8,128)S(1)} %copy-done.4, f32[1,256]{1,0:T(1,128)S(1)} %bitcast.7, ...), custom_call_target="tpu_custom_call" | custom-call | flops 2147483648 | bytes 1048576 | tf_op jit(solution)/shard_map/last/pallas_call | solution.py:199
  (26 shorter events, 0.1 us)
Async XLA Ops:
  0.1 1.2 %copy-start = (f32[1024,256]{1,0:T(8,128)S(1)}, f32[1024,256]{1,0:T(8,128)}, u32[]{:S(2)}) copy-start(f32[1024,256]{1,0:T(8,128)} %features.5) | copy-start | bytes 3145732
  1.3 0.9 %copy-start.2 = (bf16[128,1024]{1,0:T(8,128)(2,1)S(1)}, bf16[128,1024]{1,0:T(8,128)(2,1)}, u32[]{:S(2)}) copy-start(bf16[128,1024]{1,0:T(8,128)(2,1)} %hub.3) | copy-start | bytes 786436
  3.1 10.9 %collective-permute-start = (f32[32,256]{1,0:T(8,128)S(1)}, f32[32,256]{1,0:T(8,128)S(1)}, u32[]{:S(2)}, u32[]{:S(2)}) collective-permute-start(f32[32,256]{1,0:T(8,128)S(1)} %get-tuple-element.23), channel_id=1, source_target_pairs={{0,8},{8,0},{16,24},{24,16},{1,9},{9,1},{17,25},{25,17},{2,10},{10... | collective-permute-start | bytes 98312 | tf_op jit(solution)/shard_map/ppermute | solution.py:171
  6.2 7.9 %collective-permute-start.1 = (f32[32,256]{1,0:T(8,128)S(1)}, f32[32,256]{1,0:T(8,128)S(1)}, u32[]{:S(2)}, u32[]{:S(2)}) collective-permute-start(f32[32,256]{1,0:T(8,128)S(1)} %get-tuple-element.24), channel_id=1, source_target_pairs={{0,16},{8,24},{16,0},{24,8},{1,17},{9,25},{17,1},{25,9},{2,18},{10... | collective-permute-start | bytes 98312 | tf_op jit(solution)/shard_map/ppermute | solution.py:171
  8.8 4.7 %copy-start.3 = (s32[1024]{0:T(1024)S(1)}, s32[1024]{0:T(1024)}, u32[]{:S(2)}) copy-start(s32[1024]{0:T(1024)} %param.12) | copy-start | bytes 12292
  8.8 14.6 %copy-start.1 = (f32[1024,256]{1,0:T(8,128)S(1)}, f32[1024,256]{1,0:T(8,128)}, u32[]{:S(2)}) copy-start(f32[1024,256]{1,0:T(8,128)} %features.5) | copy-start | bytes 3145732
  8.8 7.1 %collective-permute-start.2 = (f32[32,256]{1,0:T(8,128)S(1)}, f32[32,256]{1,0:T(8,128)S(1)}, u32[]{:S(2)}, u32[]{:S(2)}) collective-permute-start(f32[32,256]{1,0:T(8,128)S(1)} %get-tuple-element.25), channel_id=1, source_target_pairs={{0,24},{8,16},{16,8},{24,0},{1,25},{9,17},{17,9},{25,1},{2,26},{10... | collective-permute-start | bytes 98312 | tf_op jit(solution)/shard_map/ppermute | solution.py:171
  8.8 0.8 %copy-start.5 = (s32[8,128]{1,0:T(8,128)S(1)}, s32[8,128]{1,0:T(8,128)}, u32[]{:S(2)}) copy-start(s32[8,128]{1,0:T(8,128)} %halo.1) | copy-start | bytes 12292
  9.6 3.9 %copy-start.12 = (s32[1024,16]{0,1:T(8,128)S(1)}, s32[1024,16]{0,1:T(8,128)}, u32[]{:S(2)}) copy-start(s32[1024,16]{0,1:T(8,128)} %param.11) | copy-start | bytes 196612
  11.6 8.9 %collective-permute-start.3 = (f32[128,256]{1,0:T(8,128)S(1)}, f32[128,256]{1,0:T(8,128)S(1)}, u32[]{:S(2)}, u32[]{:S(2)}) collective-permute-start(f32[128,256]{1,0:T(8,128)S(1)} %get-tuple-element.26), channel_id=1, source_target_pairs={{0,1},{1,0},{2,3},{3,2},{4,5},{5,4},{6,7},{7,6},{8,9},{9,8},{10,11... | collective-permute-start | bytes 393224 | tf_op jit(solution)/shard_map/ppermute | solution.py:155
  11.7 11.7 %collective-permute-start.4 = (f32[128,256]{1,0:T(8,128)S(1)}, f32[128,256]{1,0:T(8,128)S(1)}, u32[]{:S(2)}, u32[]{:S(2)}) collective-permute-start(f32[128,256]{1,0:T(8,128)S(1)} %get-tuple-element.27), channel_id=1, source_target_pairs={{0,2},{1,3},{2,0},{3,1},{4,6},{5,7},{6,4},{7,5},{8,10},{9,11},{10,... | collective-permute-start | bytes 393224 | tf_op jit(solution)/shard_map/ppermute | solution.py:155
  14.0 18.3 %collective-permute-start.5 = (f32[128,256]{1,0:T(8,128)S(1)}, f32[128,256]{1,0:T(8,128)S(1)}, u32[]{:S(2)}, u32[]{:S(2)}) collective-permute-start(f32[128,256]{1,0:T(8,128)S(1)} %get-tuple-element.28), channel_id=1, source_target_pairs={{0,3},{1,2},{2,1},{3,0},{4,7},{5,6},{6,5},{7,4},{8,11},{9,10},{10,... | collective-permute-start | bytes 393224 | tf_op jit(solution)/shard_map/ppermute | solution.py:155
  14.1 18.2 %collective-permute-start.6 = (f32[128,256]{1,0:T(8,128)S(1)}, f32[128,256]{1,0:T(8,128)S(1)}, u32[]{:S(2)}, u32[]{:S(2)}) collective-permute-start(f32[128,256]{1,0:T(8,128)S(1)} %get-tuple-element.29), channel_id=1, source_target_pairs={{0,4},{1,5},{2,6},{3,7},{4,0},{5,1},{6,2},{7,3},{8,12},{9,13},{10,... | collective-permute-start | bytes 393224 | tf_op jit(solution)/shard_map/ppermute | solution.py:155
  15.9 16.4 %collective-permute-start.7 = (f32[128,256]{1,0:T(8,128)S(1)}, f32[128,256]{1,0:T(8,128)S(1)}, u32[]{:S(2)}, u32[]{:S(2)}) collective-permute-start(f32[128,256]{1,0:T(8,128)S(1)} %get-tuple-element.30), channel_id=1, source_target_pairs={{0,5},{1,4},{2,7},{3,6},{4,1},{5,0},{6,3},{7,2},{8,13},{9,12},{10,... | collective-permute-start | bytes 393224 | tf_op jit(solution)/shard_map/ppermute | solution.py:155
  16.5 15.8 %all-to-all-start = ((f32[8,4,256]{2,1,0:T(4,128)}), f32[8,4,256]{2,1,0:T(4,128)S(1)}, u32[]{:S(2)}, u32[]{:S(2)}) async-start(f32[8,4,256]{2,1,0:T(4,128)} %reshape.19), calls=%async_computation | async-start | bytes 65536 | tf_op jit(solution)/shard_map/all_to_all | solution.py:174
  20.5 11.9 %collective-permute-start.8 = (f32[128,256]{1,0:T(8,128)S(1)}, f32[128,256]{1,0:T(8,128)S(1)}, u32[]{:S(2)}, u32[]{:S(2)}) collective-permute-start(f32[128,256]{1,0:T(8,128)S(1)} %get-tuple-element.31), channel_id=1, source_target_pairs={{0,6},{1,7},{2,4},{3,5},{4,2},{5,3},{6,0},{7,1},{8,14},{9,15},{10,... | collective-permute-start | bytes 393224 | tf_op jit(solution)/shard_map/ppermute | solution.py:155
  23.4 8.9 %collective-permute-start.9 = (f32[128,256]{1,0:T(8,128)S(1)}, f32[128,256]{1,0:T(8,128)S(1)}, u32[]{:S(2)}, u32[]{:S(2)}) collective-permute-start(f32[128,256]{1,0:T(8,128)S(1)} %get-tuple-element.32), channel_id=1, source_target_pairs={{0,7},{1,6},{2,5},{3,4},{4,3},{5,2},{6,1},{7,0},{8,15},{9,14},{10,... | collective-permute-start | bytes 393224 | tf_op jit(solution)/shard_map/ppermute | solution.py:155
  23.4 8.9 %copy-start.4 = (f32[256,256]{1,0:T(8,128)S(1)}, f32[256,256]{1,0:T(8,128)}, u32[]{:S(2)}) copy-start(f32[256,256]{1,0:T(8,128)} %weight.1) | copy-start | bytes 786436
  23.4 8.9 %copy-start.6 = (f32[256]{0:T(256)S(1)}, f32[256]{0:T(256)}, u32[]{:S(2)}) copy-start(f32[256]{0:T(256)} %param.15) | copy-start | bytes 3076
  23.4 8.9 %copy-start.7 = (s32[4]{0:T(128)S(1)}, s32[4]{0:T(128)}, u32[]{:S(2)}) copy-start(s32[4]{0:T(128)} %slot.1) | copy-start | bytes 52
  30.1 1.3 %copy-start.8 = (bf16[1024,896]{1,0:T(8,128)(2,1)}, bf16[1024,896]{1,0:T(8,128)(2,1)S(1)}, u32[]{:S(2)}) copy-start(bf16[1024,896]{1,0:T(8,128)(2,1)S(1)} %get-tuple-element.20.adj) | copy-start | bytes 5505028
  31.3 1.0 %copy-start.10 = (f32[1024,256]{1,0:T(8,128)}, f32[1024,256]{1,0:T(8,128)S(1)}, u32[]{:S(2)}) copy-start(f32[1024,256]{1,0:T(8,128)S(1)} %get-tuple-element.21.base) | copy-start | bytes 3145732
  32.4 1.5 %copy-start.9 = (bf16[1024,896]{1,0:T(8,128)(2,1)S(1)}, bf16[1024,896]{1,0:T(8,128)(2,1)}, u32[]{:S(2)}) copy-start(bf16[1024,896]{1,0:T(8,128)(2,1)} %copy-done.8) | copy-start | bytes 5505028
  33.9 1.2 %copy-start.11 = (f32[1024,256]{1,0:T(8,128)S(1)}, f32[1024,256]{1,0:T(8,128)}, u32[]{:S(2)}) copy-start(f32[1024,256]{1,0:T(8,128)} %copy-done.10) | copy-start | bytes 3145732
where the time goes:
time: 40.5 us; the launch traced here: 40.2 us
  starting transfers between devices  16.3 us (40%)
  Pallas kernels  14.5 us (36%)
  local copies, waits for them, and re-layouts  8.96 us (22%)
    unnamed x26, local copies, waits for them, and re-layouts  7.9 us
    ppermute x7, starting transfers between devices, on_device(): received.append(lax.ppermute(outgoing[s], 'loc', pairs))  6.69 us
    pallas_call x1, Pallas kernels, on_device(): pl.pallas_call(functools.partial(count_kernel, degree=degree, pool=pool),...  6.64 us
    ppermute x3, starting transfers between devices, on_device(): arrived = lax.ppermute(parts[s], 'grp', pairs)  5.71 us
    pallas_call x1, Pallas kernels, on_device(): pl.pallas_call(last_kernel, out_shape=jax.ShapeDtypeStruct((own, width),...  5.09 us
    all_to_all x1, starting transfers between devices, on_device(): lax.all_to_all(group_part, 'loc', split_axis=0, concat_axis=0, tiled=True)  3.91 us
    pallas_call x1, Pallas kernels, on_device(): pl.pallas_call(functools.partial(pick_kernel, peers=n_loc, rows=listed),...  2.02 us
  transfers between devices with their start and end apart: 11, of which 0 were waited for; matrix products, arithmetic and copies ran while one was open for 3% of the time, Pallas kernels for 22%

commit v1 on v0

v1 whole, which is shorter than its diff:
```python
import functools

import jax
import jax.numpy as jnp
from jax import lax
from jax.experimental import pallas as pl
from jax.experimental.pallas import tpu as pltpu
from jax.sharding import PartitionSpec as P


BF = jnp.bfloat16
F32 = jnp.float32
LANES = 128
STEPS = 4
GROUP = 16


def FLOW(peers):
    return sorted(range(1, peers), key=lambda s: (s < 2, s & 1, -s)) + [0]


def split(x):
    hi = x.astype(BF)
    return hi, (x - hi.astype(F32)).astype(BF)


def mm(a, b, dims=((1,), (0,))):
    return lax.dot_general(a, b, (dims, ((), ())), preferred_element_type=F32)


def pick_kernel(me, features, halo, *refs, peers, rows):
    outs, order = refs[:peers], refs[peers]
    hi, lo = split(features[...])
    own = features.shape[0]
    for s in range(peers):
        order[s : s + 1, :] = halo[pl.ds(me[1] ^ s, 1), :]
    listed = order[...].T
    col = lax.broadcasted_iota(jnp.int32, (rows, own), 1)
    for s in FLOW(peers):
        hot = (listed[:, s : s + 1] == col).astype(F32).astype(BF)
        outs[s][...] = mm(hot, hi) + mm(hot, lo)


def hub_kernel(me, features, hub, *refs, parts):
    outs, full = refs[:parts], refs[parts]
    full[...] = mm(hub[...], features[...].astype(BF))
    size = full.shape[0] // parts
    for s in range(parts):
        at = pl.multiple_of((me[0] ^ s) * size, size)
        outs[s][...] = full[pl.ds(at, size), :]


def inverse_counts(counts):
    return 1.0 / counts[...].astype(F32).T


def count_kernel(me, features, mine, names, counts, adj, base, code_s, low_s, near_s, far_s, base_s, sems):
    own, _ = features.shape
    degree = names.shape[0]
    listed = mine.shape[0]
    tiles = own // LANES
    span = GROUP * degree
    each = LANES // GROUP
    near, far = near_s.shape[1] // LANES, far_s.shape[1] // LANES
    codes = near + far

    stacked = jnp.concatenate(
        [names[:, j * LANES : (j + 1) * LANES] for j in range(tiles)], axis=0
    )
    limit = jnp.concatenate(
        [jnp.broadcast_to(counts[j : j + 1, :], (degree, LANES)) for j in range(tiles)], axis=0
    )
    spot = lax.broadcasted_iota(jnp.int32, stacked.shape, 0) % degree
    away = stacked - own
    moved = own + ((away // listed) ^ me[1]) * listed + away % listed
    named = jnp.where(stacked < own, stacked, moved)
    code = jnp.where(spot < limit, named // LANES, -1).astype(F32).astype(BF)
    low = (named % LANES).astype(F32).astype(BF)
    wide = (LANES, each * span)
    lane = lax.broadcasted_iota(jnp.int32, wide, 1)
    vertex = lax.broadcasted_iota(jnp.int32, wide, 0)
    choose = (vertex == (lane // span) * GROUP + lane % GROUP).astype(F32).astype(BF)
    rows = (tiles * degree, each * span)
    lane = lax.broadcasted_iota(jnp.int32, rows, 1)
    kept = lax.broadcasted_iota(jnp.int32, rows, 0) % degree == (lane % span) // GROUP

    def line_up(x):
        spread = jnp.where(kept, mm(x, choose), 0.0)
        return jnp.sum(spread.reshape(tiles, degree, each * span), axis=1)

    member = (lax.broadcasted_iota(jnp.int32, (1, each * span), 1) % GROUP).astype(F32)
    code_s[...] = line_up(code) * GROUP + member
    low_s[...] = line_up(low)

    kind = BF if codes * GROUP <= 256 else F32
    row = lax.broadcasted_iota(jnp.int32, (codes * GROUP, span), 0).astype(F32).astype(kind)
    bits = lax.broadcasted_iota(jnp.int32, (LANES, span), 0).astype(F32).astype(BF)

    def hot(x, y):
        return jnp.where(x == y, jnp.ones((), x.dtype), jnp.zeros((), x.dtype)).astype(BF)

    def build(j, _):
        for e in range(each):
            cut = slice(e * span, (e + 1) * span)
            left = hot(row, code_s[pl.ds(j, 1), cut].astype(kind))
            right = hot(bits, low_s[pl.ds(j, 1), cut].astype(BF))
            made = mm(left, right, ((1,), (1,))).astype(BF)
            at = pl.multiple_of(j * LANES + e * GROUP, GROUP)
            for h in range(codes):
                part = made[h * GROUP : (h + 1) * GROUP]
                to, k = (near_s, h) if h < near else (far_s, h - near)
                to[pl.ds(at, GROUP), k * LANES : (k + 1) * LANES] = part
        return 0

    lax.fori_loop(0, tiles, build, 0)
    first = pltpu.make_async_copy(far_s, adj, sems.at[0])
    first.start()
    hi, lo = split(jnp.concatenate([features[...], mine[...]], axis=0))
    inv = inverse_counts(counts)
    for j in range(tiles):
        cut = slice(j * LANES, (j + 1) * LANES)
        a = near_s[cut, :]
        base_s[cut, :] = features[cut, :] + (mm(a, hi) + mm(a, lo)) * inv[:, j : j + 1]
    second = pltpu.make_async_copy(base_s, base, sems.at[1])
    second.start()
    first.wait()
    second.wait()


def last_kernel(slot, adj, base, counts, hub, weight, bias, *refs):
    pieces, (out, adj_s, base_s, out_s, rhi, rlo, ins, ends) = refs[:-8], refs[-8:]
    size = pieces[0].shape[0]
    rows = adj_s.shape[0] // STEPS
    cuts = [pl.ds(n * rows, rows) for n in range(STEPS)]
    loads = []
    for n, cut in enumerate(cuts):
        loads.append(pltpu.make_async_copy(adj.at[cut], adj_s.at[cut], ins.at[2 * n]))
        loads.append(pltpu.make_async_copy(base.at[cut], base_s.at[cut], ins.at[2 * n + 1]))
    for load in loads:
        load.start()
    for n, piece in enumerate(pieces):
        cut = slice(n * size, (n + 1) * size)
        rhi[cut, :], rlo[cut, :] = split(piece[...])
    whi, wlo = split(weight[...])
    inv = inverse_counts(counts)
    sums = jnp.sum(hub[...], axis=0)
    per = rows // LANES
    stores = []
    for n, cut in enumerate(cuts):
        loads[2 * n].wait()
        loads[2 * n + 1].wait()
        a = adj_s[cut, :]
        summed = mm(a, rhi[...]) + mm(a, rlo[...])
        scale = jnp.concatenate([inv[:, n * per + j : n * per + j + 1] for j in range(per)], axis=0)
        comb = base_s[cut, :] + summed * scale
        row = lax.broadcasted_iota(jnp.int32, (rows, 1), 0) + n * rows
        for i in range(sums.shape[0]):
            comb = comb + jnp.where(row == slot[i], sums[i : i + 1], 0.0)
        chi, clo = split(comb)
        made = mm(chi, whi) + (mm(chi, wlo) + mm(clo, whi)) + bias[...]
        out_s[cut, :] = jnp.maximum(made, 0.0)
        store = pltpu.make_async_copy(out_s.at[cut], out.at[cut], ends.at[n])
        store.start()
        stores.append(store)
    for store in stores:
        store.wait()


VMEM = pl.BlockSpec(memory_space=pltpu.VMEM)
HBM = pl.BlockSpec(memory_space=pltpu.HBM)
SMEM = pl.BlockSpec(memory_space=pltpu.SMEM)
PARAMS = pltpu.CompilerParams(vmem_limit_bytes=24 * 1024 * 1024)


def flops(n):
    return pl.CostEstimate(flops=n, bytes_accessed=1 << 20, transcendentals=0)


def on_device(features, hub_block, hub_slot, neighbours, counts, halo_send, weight, bias):
    own, width = features.shape
    degree = neighbours.shape[1]
    n_grp, n_loc = lax.axis_size("grp"), lax.axis_size("loc")
    listed = halo_send.shape[1]
    hubs = hub_block.shape[0]
    owned = hub_slot.shape[0]
    pool = own + n_loc * listed
    here = lax.axis_index("loc").astype(jnp.int32)
    me = jnp.stack([lax.axis_index("grp").astype(jnp.int32), here])

    outgoing = pl.pallas_call(
        functools.partial(pick_kernel, peers=n_loc, rows=listed),
        out_shape=[jax.ShapeDtypeStruct((listed, width), F32)] * n_loc,
        in_specs=[SMEM] + [VMEM] * 2,
        out_specs=[VMEM] * n_loc,
        scratch_shapes=[pltpu.VMEM((n_loc, listed), jnp.int32)],
        compiler_params=PARAMS,
        cost_estimate=flops(4 * n_loc * listed * own * width),
        name="pick",
    )(me, features, halo_send)
    received = []
    for s in range(1, n_loc):
        pairs = [(i, i ^ s) for i in range(n_loc)]
        received.append(lax.ppermute(outgoing[s], "loc", pairs))

    part_rows = hubs // n_grp
    parts = pl.pallas_call(
        functools.partial(hub_kernel, parts=n_grp),
        out_shape=[jax.ShapeDtypeStruct((part_rows, width), F32)] * n_grp,
        in_specs=[SMEM, VMEM, VMEM],
        out_specs=[VMEM] * n_grp,
        scratch_shapes=[pltpu.VMEM((hubs, width), F32)],
        compiler_params=PARAMS,
        cost_estimate=flops(2 * hubs * own * width),
        name="hub",
    )(me, features, hub_block)
    group_part = parts[0]
    for s in range(1, n_grp):
        pairs = [(i, i ^ s) for i in range(n_grp)]
        arrived = lax.ppermute(parts[s], "grp", pairs)
        group_part = group_part + arrived
    group_part = group_part.reshape(n_loc, owned, width)
    hub_pieces = lax.all_to_all(group_part, "loc", split_axis=0, concat_axis=0, tiled=True)

    remote = pool - own - listed
    tiles = own // LANES
    counts_rows = counts.reshape(tiles, LANES)
    line = (tiles, LANES * degree)
    adj, base = pl.pallas_call(
        count_kernel,
        out_shape=[
            pltpu.HBM((own, remote), BF),
            pltpu.HBM((own, width), F32),
        ],
        in_specs=[SMEM] + [VMEM] * 4,
        out_specs=[HBM] * 2,
        scratch_shapes=[
            pltpu.VMEM(line, F32),
            pltpu.VMEM(line, F32),
            pltpu.VMEM((own, own + listed), BF),
            pltpu.VMEM((own, remote), BF),
            pltpu.VMEM((own, width), F32),
            pltpu.SemaphoreType.DMA((2,)),
        ],
        compiler_params=PARAMS,
        cost_estimate=flops(8 * own * own * width),
        name="count",
    )(me, features, outgoing[0], neighbours.T, counts_rows)

    adj = pltpu.with_memory_space_constraint(adj, pltpu.HBM)
    base = pltpu.with_memory_space_constraint(base, pltpu.HBM)
    return pl.pallas_call(
        last_kernel,
        out_shape=jax.ShapeDtypeStruct((own, width), F32),
        in_specs=[SMEM, HBM, HBM] + [VMEM] * (4 + len(received)),
        out_specs=HBM,
        scratch_shapes=[
            pltpu.VMEM((own, remote), BF),
            pltpu.VMEM((own, width), F32),
            pltpu.VMEM((own, width), F32),
            pltpu.VMEM((remote, width), BF),
            pltpu.VMEM((remote, width), BF),
            pltpu.SemaphoreType.DMA((2 * STEPS,)),
            pltpu.SemaphoreType.DMA((STEPS,)),
        ],
        compiler_params=PARAMS,
        cost_estimate=flops(8 * own * own * width),
        name="last",
    )(
        hub_slot, adj, base, counts_rows, hub_pieces, weight, bias.reshape(1, width), *received
    )


def solution(mesh):
    in_specs = (
        P(("grp", "loc"), None),
        P(None, ("grp", "loc")),
        P(("grp", "loc")),
        P(("grp", "loc"), None),
        P(("grp", "loc")),
        P(("grp", "loc"), None),
        P(),
        P(),
    )
    out_specs = P(("grp", "loc"), None)
    return jax.shard_map(
        on_device, mesh=mesh, in_specs=in_specs, out_specs=out_specs, check_vma=False
    )
```

time: 40.5 us -> 37.1 us (0.916)
  local copies, waits for them, and re-layouts: 8.96 us -> 3.6 us
  Pallas kernels: 14.5 us -> 16.7 us
    unnamed x26 -> x18, local copies, waits for them, and re-layouts: 7.9 us -> 2.98 us
    pallas_call x1, Pallas kernels: 5.09 us -> 6.35 us  [on_device(): pl.pallas_call(last_kernel, out_shape=jax.ShapeDtypeStruct((own, width),...]
    pallas_call x1, Pallas kernels: 6.64 us -> 7.54 us  [on_device(): pl.pallas_call(count_kernel, out_shape=[pltpu.HBM((own, remote), BF), plt...]
  transfers between devices with their start and end apart: 11 -> 11, of which waited for: 0 -> 0; matrix products, arithmetic and copies ran while one was open for 3% -> 2% of each run, Pallas kernels for 22% -> 26%
where the time goes in v1:
time: 37.1 us; the launch traced here: 36.8 us
  Pallas kernels  16.7 us (45%)
  starting transfers between devices  16.3 us (44%)
  local copies, waits for them, and re-layouts  3.6 us (10%)
    pallas_call x1, Pallas kernels, on_device(): pl.pallas_call(count_kernel, out_shape=[pltpu.HBM((own, remote), BF), plt...  7.54 us
    ppermute x7, starting transfers between devices, on_device(): received.append(lax.ppermute(outgoing[s], 'loc', pairs))  6.63 us
    pallas_call x1, Pallas kernels, on_device(): pl.pallas_call(last_kernel, out_shape=jax.ShapeDtypeStruct((own, width),...  6.35 us
    ppermute x3, starting transfers between devices, on_device(): arrived = lax.ppermute(parts[s], 'grp', pairs)  5.71 us
    all_to_all x1, starting transfers between devices, on_device(): lax.all_to_all(group_part, 'loc', split_axis=0, concat_axis=0, tiled=True)  3.92 us
    unnamed x18, local copies, waits for them, and re-layouts  2.98 us
    pallas_call x1, Pallas kernels, on_device(): pl.pallas_call(functools.partial(pick_kernel, peers=n_loc, rows=listed),...  2.02 us
    pallas_call x1, Pallas kernels, on_device(): pl.pallas_call(functools.partial(hub_kernel, parts=n_grp), out_shape=[jax...  0.78 us
  transfers between devices with their start and end apart: 11, of which 0 were waited for; matrix products, arithmetic and copies ran while one was open for 2% of the time, Pallas kernels for 26%

profile of v1, /device:TPU:0, one launch (start us, length us, event | category | flops | bytes accessed | tf_op | source)
XLA Modules:
  0.0 36.8 jit_solution(641033944371582461)
XLA Ops:
  0.0 0.1 pad_add_fusion.me
  0.1 1.2 %copy-done = f32[1024,256]{1,0:T(8,128)S(1)} copy-done((f32[1024,256]{1,0:T(8,128)S(1)}, f32[1024,256]{1,0:T(8,128)}, u32[]{:S(2)}) %copy-start) | copy-done | bytes 1048600
  1.3 0.9 %copy-done.2 = bf16[128,1024]{1,0:T(8,128)(2,1)S(1)} copy-done((bf16[128,1024]{1,0:T(8,128)(2,1)S(1)}, bf16[128,1024]{1,0:T(8,128)(2,1)}, u32[]{:S(2)}) %copy-start.2) | copy-done | bytes 262168
  2.3 0.8 %hub.2 = (f32[32,256]{1,0:T(8,128)S(1)}, f32[32,256]{1,0:T(8,128)S(1)}, f32[32,256]{1,0:T(8,128)S(1)}, f32[32,256]{1,0:T(8,128)S(1)}) custom-call(s32[2]{0:T(128)S(1)} %pad_add_fusion.me, f32[1024,256]{1,0:T(8,128)S(1)} %copy-done, bf16[128,1024]{1,0:T(8,128)(2,1)S(1)} %copy-done.2), custom_call_target="tpu_custom_call" | custom-call | flops 67108864 | bytes 1048576 | tf_op jit(solution)/shard_map/hub/pallas_call | solution.py:206
  3.0 3.1 %collective-permute-start = (f32[32,256]{1,0:T(8,128)S(1)}, f32[32,256]{1,0:T(8,128)S(1)}, u32[]{:S(2)}, u32[]{:S(2)}) collective-permute-start(f32[32,256]{1,0:T(8,128)S(1)} %get-tuple-element.23), channel_id=1, source_target_pairs={{0,8},{8,0},{16,24},{24,16},{1,9},{9,1},{17,25},{25,17},{2,10},{10... | collective-permute-start | bytes 98312 | tf_op jit(solution)/shard_map/ppermute | solution.py:219
  6.2 2.6 %collective-permute-start.1 = (f32[32,256]{1,0:T(8,128)S(1)}, f32[32,256]{1,0:T(8,128)S(1)}, u32[]{:S(2)}, u32[]{:S(2)}) collective-permute-start(f32[32,256]{1,0:T(8,128)S(1)} %get-tuple-element.24), channel_id=1, source_target_pairs={{0,16},{8,24},{16,0},{24,8},{1,17},{9,25},{17,1},{25,9},{2,18},{10... | collective-permute-start | bytes 98312 | tf_op jit(solution)/shard_map/ppermute | solution.py:219
  8.8 0.0 collective-permute-start.2
  8.8 0.8 %copy-done.5 = s32[8,128]{1,0:T(8,128)S(1)} copy-done((s32[8,128]{1,0:T(8,128)S(1)}, s32[8,128]{1,0:T(8,128)}, u32[]{:S(2)}) %copy-start.5) | copy-done | bytes 4120
  9.5 2.0 %pick.1 = (f32[128,256]{1,0:T(8,128)S(1)}, f32[128,256]{1,0:T(8,128)S(1)}, f32[128,256]{1,0:T(8,128)S(1)}, f32[128,256]{1,0:T(8,128)S(1)}, f32[128,256]{1,0:T(8,...) custom-call(s32[2]{0:T(128)S(1)} %pad_add_fusion.me, f32[1024,256]{1,0:T(8,128)S(1)} %copy-done, ...), custom_call_target="tpu_custom_call" | custom-call | flops 1073741824 | bytes 1048576 | tf_op jit(solution)/shard_map/pick/pallas_call | solution.py:190
  11.6 0.1 collective-permute-start.3
  11.6 1.8 %collective-permute-start.4 = (f32[128,256]{1,0:T(8,128)S(1)}, f32[128,256]{1,0:T(8,128)S(1)}, u32[]{:S(2)}, u32[]{:S(2)}) collective-permute-start(f32[128,256]{1,0:T(8,128)S(1)} %get-tuple-element.27), channel_id=1, source_target_pairs={{0,2},{1,3},{2,0},{3,1},{4,6},{5,7},{6,4},{7,5},{8,10},{9,11},{10,... | collective-permute-start | bytes 393224 | tf_op jit(solution)/shard_map/ppermute | solution.py:203
  13.4 0.0 collective-permute-done
  13.4 0.1 collective-permute-start.5
  13.5 0.0 collective-permute-done.1
  13.5 1.8 %collective-permute-start.6 = (f32[128,256]{1,0:T(8,128)S(1)}, f32[128,256]{1,0:T(8,128)S(1)}, u32[]{:S(2)}, u32[]{:S(2)}) collective-permute-start(f32[128,256]{1,0:T(8,128)S(1)} %get-tuple-element.29), channel_id=1, source_target_pairs={{0,4},{1,5},{2,6},{3,7},{4,0},{5,1},{6,2},{7,3},{8,12},{9,13},{10,... | collective-permute-start | bytes 393224 | tf_op jit(solution)/shard_map/ppermute | solution.py:203
  15.3 0.0 collective-permute-done.2
  15.3 0.0 collective-permute-start.7
  15.3 0.6 %reshape.10 = f32[8,4,256]{2,1,0:T(4,128)} reshape(f32[32,256]{1,0:T(8,128)S(1)} %add_add_fusion) | data formatting | bytes 65536 | tf_op jit(solution)/shard_map/reshape | solution.py:221
  15.9 3.9 %all-to-all-start = ((f32[8,4,256]{2,1,0:T(4,128)}), f32[8,4,256]{2,1,0:T(4,128)S(1)}, u32[]{:S(2)}, u32[]{:S(2)}) async-start(f32[8,4,256]{2,1,0:T(4,128)} %reshape.10), calls=%async_computation | async-start | bytes 65536 | tf_op jit(solution)/shard_map/all_to_all | solution.py:222
  19.8 0.0 collective-permute-done.3.refs_0_
  19.9 2.9 %collective-permute-start.8 = (f32[128,256]{1,0:T(8,128)S(1)}, f32[128,256]{1,0:T(8,128)S(1)}, u32[]{:S(2)}, u32[]{:S(2)}) collective-permute-start(f32[128,256]{1,0:T(8,128)S(1)} %get-tuple-element.31), channel_id=1, source_target_pairs={{0,6},{1,7},{2,4},{3,5},{4,2},{5,3},{6,0},{7,1},{8,14},{9,15},{10,... | collective-permute-start | bytes 393224 | tf_op jit(solution)/shard_map/ppermute | solution.py:203
  22.8 0.0 collective-permute-done.4.refs_1_
  22.8 0.0 collective-permute-start.9
  22.8 0.0 copy-start.3
  22.8 0.0 copy-start.7
  22.8 0.0 copy-start.8
  22.8 7.5 %count.1 = (bf16[1024,896]{1,0:T(8,128)(2,1)}, f32[1024,256]{1,0:T(8,128)}) custom-call(s32[2]{0:T(128)S(1)} %pad_add_fusion.me, f32[1024,256]{1,0:T(8,128)S(1)} %copy-done.1, f32[128,256]{1,0:T(8,128)S(1)} %get-tuple-element.19.mine, s32[16,1024]{1,0:T(8,128)S(1)} %bitcast.5, s32[8,128]{1,0:T(8,128)S(1)} %bitcast.6), custom_call_target="tpu_custom_call" | custom-call | flops 2147483648 | bytes 1048576 | tf_op jit(solution)/shard_map/count/pallas_call | solution.py:228
  30.4 0.0 all-to-all-done.hub
  30.4 0.0 collective-permute-done.5.refs_2_
  30.4 0.0 collective-permute-done.8.refs_5_
  30.4 0.0 collective-permute-done.9.refs_6_
  30.5 6.4 %last.1 = f32[1024,256]{1,0:T(8,128)} custom-call(s32[4]{0:T(128)S(1)} %copy-done.8, bf16[1024,896]{1,0:T(8,128)(2,1)} %get-tuple-element.20.adj, f32[1024,256]{1,0:T(8,128)} %get-tuple-element.21.base, s32[8,128]{1,0:T(8,128)S(1)} %bitcast.7, f32[8,4,256]{2,1,0:T(4,128)S(1)} %all-to-all-done.hub, f32[256,256]{1,0:T(8,128)S(1)} %copy-done.3, ...), custom_call_target="tpu_custom_call" | custom-call | flops 2147483648 | bytes 1048576 | tf_op jit(solution)/shard_map/last/pallas_call | solution.py:251
  (15 shorter events, 0.0 us)
Async XLA Ops:
  0.1 1.2 %copy-start = (f32[1024,256]{1,0:T(8,128)S(1)}, f32[1024,256]{1,0:T(8,128)}, u32[]{:S(2)}) copy-start(f32[1024,256]{1,0:T(8,128)} %features.5) | copy-start | bytes 3145732
  1.3 0.9 %copy-start.2 = (bf16[128,1024]{1,0:T(8,128)(2,1)S(1)}, bf16[128,1024]{1,0:T(8,128)(2,1)}, u32[]{:S(2)}) copy-start(bf16[128,1024]{1,0:T(8,128)(2,1)} %hub.3) | copy-start | bytes 786436
  3.0 10.4 %collective-permute-start = (f32[32,256]{1,0:T(8,128)S(1)}, f32[32,256]{1,0:T(8,128)S(1)}, u32[]{:S(2)}, u32[]{:S(2)}) collective-permute-start(f32[32,256]{1,0:T(8,128)S(1)} %get-tuple-element.23), channel_id=1, source_target_pairs={{0,8},{8,0},{16,24},{24,16},{1,9},{9,1},{17,25},{25,17},{2,10},{10... | collective-permute-start | bytes 98312 | tf_op jit(solution)/shard_map/ppermute | solution.py:219
  6.2 7.3 %collective-permute-start.1 = (f32[32,256]{1,0:T(8,128)S(1)}, f32[32,256]{1,0:T(8,128)S(1)}, u32[]{:S(2)}, u32[]{:S(2)}) collective-permute-start(f32[32,256]{1,0:T(8,128)S(1)} %get-tuple-element.24), channel_id=1, source_target_pairs={{0,16},{8,24},{16,0},{24,8},{1,17},{9,25},{17,1},{25,9},{2,18},{10... | collective-permute-start | bytes 98312 | tf_op jit(solution)/shard_map/ppermute | solution.py:219
  8.8 14.0 %copy-start.1 = (f32[1024,256]{1,0:T(8,128)S(1)}, f32[1024,256]{1,0:T(8,128)}, u32[]{:S(2)}) copy-start(f32[1024,256]{1,0:T(8,128)} %features.5) | copy-start | bytes 3145732
  8.8 14.0 %copy-start.4 = (s32[1024,16]{0,1:T(8,128)S(1)}, s32[1024,16]{0,1:T(8,128)}, u32[]{:S(2)}) copy-start(s32[1024,16]{0,1:T(8,128)} %param.11) | copy-start | bytes 196612
  8.8 6.5 %collective-permute-start.2 = (f32[32,256]{1,0:T(8,128)S(1)}, f32[32,256]{1,0:T(8,128)S(1)}, u32[]{:S(2)}, u32[]{:S(2)}) collective-permute-start(f32[32,256]{1,0:T(8,128)S(1)} %get-tuple-element.25), channel_id=1, source_target_pairs={{0,24},{8,16},{16,8},{24,0},{1,25},{9,17},{17,9},{25,1},{2,26},{10... | collective-permute-start | bytes 98312 | tf_op jit(solution)/shard_map/ppermute | solution.py:219
  8.8 0.8 %copy-start.5 = (s32[8,128]{1,0:T(8,128)S(1)}, s32[8,128]{1,0:T(8,128)}, u32[]{:S(2)}) copy-start(s32[8,128]{1,0:T(8,128)} %halo.1) | copy-start | bytes 12292
  9.5 13.3 %copy-start.6 = (s32[1024]{0:T(1024)S(1)}, s32[1024]{0:T(1024)}, u32[]{:S(2)}) copy-start(s32[1024]{0:T(1024)} %param.12) | copy-start | bytes 12292
  11.6 8.3 %collective-permute-start.3 = (f32[128,256]{1,0:T(8,128)S(1)}, f32[128,256]{1,0:T(8,128)S(1)}, u32[]{:S(2)}, u32[]{:S(2)}) collective-permute-start(f32[128,256]{1,0:T(8,128)S(1)} %get-tuple-element.26), channel_id=1, source_target_pairs={{0,1},{1,0},{2,3},{3,2},{4,5},{5,4},{6,7},{7,6},{8,9},{9,8},{10,11... | collective-permute-start | bytes 393224 | tf_op jit(solution)/shard_map/ppermute | solution.py:203
  11.6 11.1 %collective-permute-start.4 = (f32[128,256]{1,0:T(8,128)S(1)}, f32[128,256]{1,0:T(8,128)S(1)}, u32[]{:S(2)}, u32[]{:S(2)}) collective-permute-start(f32[128,256]{1,0:T(8,128)S(1)} %get-tuple-element.27), channel_id=1, source_target_pairs={{0,2},{1,3},{2,0},{3,1},{4,6},{5,7},{6,4},{7,5},{8,10},{9,11},{10,... | collective-permute-start | bytes 393224 | tf_op jit(solution)/shard_map/ppermute | solution.py:203
  13.4 17.0 %collective-permute-start.5 = (f32[128,256]{1,0:T(8,128)S(1)}, f32[128,256]{1,0:T(8,128)S(1)}, u32[]{:S(2)}, u32[]{:S(2)}) collective-permute-start(f32[128,256]{1,0:T(8,128)S(1)} %get-tuple-element.28), channel_id=1, source_target_pairs={{0,3},{1,2},{2,1},{3,0},{4,7},{5,6},{6,5},{7,4},{8,11},{9,10},{10,... | collective-permute-start | bytes 393224 | tf_op jit(solution)/shard_map/ppermute | solution.py:203
  13.5 16.9 %collective-permute-start.6 = (f32[128,256]{1,0:T(8,128)S(1)}, f32[128,256]{1,0:T(8,128)S(1)}, u32[]{:S(2)}, u32[]{:S(2)}) collective-permute-start(f32[128,256]{1,0:T(8,128)S(1)} %get-tuple-element.29), channel_id=1, source_target_pairs={{0,4},{1,5},{2,6},{3,7},{4,0},{5,1},{6,2},{7,3},{8,12},{9,13},{10,... | collective-permute-start | bytes 393224 | tf_op jit(solution)/shard_map/ppermute | solution.py:203
  15.3 15.2 %collective-permute-start.7 = (f32[128,256]{1,0:T(8,128)S(1)}, f32[128,256]{1,0:T(8,128)S(1)}, u32[]{:S(2)}, u32[]{:S(2)}) collective-permute-start(f32[128,256]{1,0:T(8,128)S(1)} %get-tuple-element.30), channel_id=1, source_target_pairs={{0,5},{1,4},{2,7},{3,6},{4,1},{5,0},{6,3},{7,2},{8,13},{9,12},{10,... | collective-permute-start | bytes 393224 | tf_op jit(solution)/shard_map/ppermute | solution.py:203
  15.9 14.5 %all-to-all-start = ((f32[8,4,256]{2,1,0:T(4,128)}), f32[8,4,256]{2,1,0:T(4,128)S(1)}, u32[]{:S(2)}, u32[]{:S(2)}) async-start(f32[8,4,256]{2,1,0:T(4,128)} %reshape.10), calls=%async_computation | async-start | bytes 65536 | tf_op jit(solution)/shard_map/all_to_all | solution.py:222
  19.9 10.6 %collective-permute-start.8 = (f32[128,256]{1,0:T(8,128)S(1)}, f32[128,256]{1,0:T(8,128)S(1)}, u32[]{:S(2)}, u32[]{:S(2)}) collective-permute-start(f32[128,256]{1,0:T(8,128)S(1)} %get-tuple-element.31), channel_id=1, source_target_pairs={{0,6},{1,7},{2,4},{3,5},{4,2},{5,3},{6,0},{7,1},{8,14},{9,15},{10,... | collective-permute-start | bytes 393224 | tf_op jit(solution)/shard_map/ppermute | solution.py:203
  22.8 7.7 %collective-permute-start.9 = (f32[128,256]{1,0:T(8,128)S(1)}, f32[128,256]{1,0:T(8,128)S(1)}, u32[]{:S(2)}, u32[]{:S(2)}) collective-permute-start(f32[128,256]{1,0:T(8,128)S(1)} %get-tuple-element.32), channel_id=1, source_target_pairs={{0,7},{1,6},{2,5},{3,4},{4,3},{5,2},{6,1},{7,0},{8,15},{9,14},{10,... | collective-permute-start | bytes 393224 | tf_op jit(solution)/shard_map/ppermute | solution.py:203
  22.8 7.6 %copy-start.3 = (f32[256,256]{1,0:T(8,128)S(1)}, f32[256,256]{1,0:T(8,128)}, u32[]{:S(2)}) copy-start(f32[256,256]{1,0:T(8,128)} %weight.1) | copy-start | bytes 786436
  22.8 7.6 %copy-start.7 = (f32[256]{0:T(256)S(1)}, f32[256]{0:T(256)}, u32[]{:S(2)}) copy-start(f32[256]{0:T(256)} %param.15) | copy-start | bytes 3076
  22.8 7.6 %copy-start.8 = (s32[4]{0:T(128)S(1)}, s32[4]{0:T(128)}, u32[]{:S(2)}) copy-start(s32[4]{0:T(128)} %slot.1) | copy-start | bytes 52

commit v2 on v1

--- a/solution.py
+++ b/solution.py
@@ -50,11 +50,23 @@
         outs[s][...] = full[pl.ds(at, size), :]
 
 
+def fold_kernel(me, *refs, parts, peers):
+    ins, outs, full = refs[:parts], refs[parts:-1], refs[-1]
+    total = ins[0][...]
+    for piece in ins[1:]:
+        total = total + piece[...]
+    full[...] = total
+    size = full.shape[0] // peers
+    for s in range(peers):
+        for i in range(size):
+            outs[s][i : i + 1, :] = full[pl.ds((me[1] ^ s) * size + i, 1), :]
+
+
 def inverse_counts(counts):
     return 1.0 / counts[...].astype(F32).T
 
 
-def count_kernel(me, features, mine, names, counts, adj, base, code_s, low_s, near_s, far_s, base_s, sems):
+def count_kernel(me, features, mine, names, counts, far_s, base, code_s, low_s, near_s):
     own, _ = features.shape
     degree = names.shape[0]
     listed = mine.shape[0]
@@ -113,46 +125,34 @@
         return 0
 
     lax.fori_loop(0, tiles, build, 0)
-    first = pltpu.make_async_copy(far_s, adj, sems.at[0])
-    first.start()
     hi, lo = split(jnp.concatenate([features[...], mine[...]], axis=0))
     inv = inverse_counts(counts)
     for j in range(tiles):
         cut = slice(j * LANES, (j + 1) * LANES)
         a = near_s[cut, :]
-        base_s[cut, :] = features[cut, :] + (mm(a, hi) + mm(a, lo)) * inv[:, j : j + 1]
-    second = pltpu.make_async_copy(base_s, base, sems.at[1])
-    second.start()
-    first.wait()
-    second.wait()
-
-
-def last_kernel(slot, adj, base, counts, hub, weight, bias, *refs):
-    pieces, (out, adj_s, base_s, out_s, rhi, rlo, ins, ends) = refs[:-8], refs[-8:]
+        base[cut, :] = features[cut, :] + (mm(a, hi) + mm(a, lo)) * inv[:, j : j + 1]
+
+
+def last_kernel(slot, adj, base, counts, weight, bias, *refs, peers):
+    hubs, pieces, (out, out_s, rhi, rlo, ends) = refs[:peers], refs[peers:-5], refs[-5:]
     size = pieces[0].shape[0]
-    rows = adj_s.shape[0] // STEPS
+    rows = adj.shape[0] // STEPS
     cuts = [pl.ds(n * rows, rows) for n in range(STEPS)]
-    loads = []
-    for n, cut in enumerate(cuts):
-        loads.append(pltpu.make_async_copy(adj.at[cut], adj_s.at[cut], ins.at[2 * n]))
-        loads.append(pltpu.make_async_copy(base.at[cut], base_s.at[cut], ins.at[2 * n + 1]))
-    for load in loads:
-        load.start()
     for n, piece in enumerate(pieces):
         cut = slice(n * size, (n + 1) * size)
         rhi[cut, :], rlo[cut, :] = split(piece[...])
     whi, wlo = split(weight[...])
     inv = inverse_counts(counts)
-    sums = jnp.sum(hub[...], axis=0)
+    sums = hubs[0][...]
+    for hub in hubs[1:]:
+        sums = sums + hub[...]
     per = rows // LANES
     stores = []
     for n, cut in enumerate(cuts):
-        loads[2 * n].wait()
-        loads[2 * n + 1].wait()
-        a = adj_s[cut, :]
+        a = adj[cut, :]
         summed = mm(a, rhi[...]) + mm(a, rlo[...])
         scale = jnp.concatenate([inv[:, n * per + j : n * per + j + 1] for j in range(per)], axis=0)
-        comb = base_s[cut, :] + summed * scale
+        comb = base[cut, :] + summed * scale
         row = lax.broadcasted_iota(jnp.int32, (rows, 1), 0) + n * rows
         for i in range(sums.shape[0]):
             comb = comb + jnp.where(row == slot[i], sums[i : i + 1], 0.0)
@@ -213,13 +213,23 @@
         cost_estimate=flops(2 * hubs * own * width),
         name="hub",
     )(me, features, hub_block)
-    group_part = parts[0]
+    arrived = [parts[0]]
     for s in range(1, n_grp):
         pairs = [(i, i ^ s) for i in range(n_grp)]
-        arrived = lax.ppermute(parts[s], "grp", pairs)
-        group_part = group_part + arrived
-    group_part = group_part.reshape(n_loc, owned, width)
-    hub_pieces = lax.all_to_all(group_part, "loc", split_axis=0, concat_axis=0, tiled=True)
+        arrived.append(lax.ppermute(parts[s], "grp", pairs))
+    folded = pl.pallas_call(
+        functools.partial(fold_kernel, parts=n_grp, peers=n_loc),
+        out_shape=[jax.ShapeDtypeStruct((owned, width), F32)] * n_loc,
+        in_specs=[SMEM] + [VMEM] * n_grp,
+        out_specs=[VMEM] * n_loc,
+        scratch_shapes=[pltpu.VMEM((part_rows, width), F32)],
+        compiler_params=PARAMS,
+        name="fold",
+    )(me, *arrived)
+    hub_pieces = [folded[0]]
+    for s in range(1, n_loc):
+        pairs = [(i, i ^ s) for i in range(n_loc)]
+        hub_pieces.append(lax.ppermute(folded[s], "loc", pairs))
 
     remote = pool - own - listed
     tiles = own // LANES
@@ -228,45 +238,37 @@
     adj, base = pl.pallas_call(
         count_kernel,
         out_shape=[
-            pltpu.HBM((own, remote), BF),
-            pltpu.HBM((own, width), F32),
+            jax.ShapeDtypeStruct((own, remote), BF),
+            jax.ShapeDtypeStruct((own, width), F32),
         ],
         in_specs=[SMEM] + [VMEM] * 4,
-        out_specs=[HBM] * 2,
+        out_specs=[VMEM] * 2,
         scratch_shapes=[
             pltpu.VMEM(line, F32),
             pltpu.VMEM(line, F32),
             pltpu.VMEM((own, own + listed), BF),
-            pltpu.VMEM((own, remote), BF),
-            pltpu.VMEM((own, width), F32),
-            pltpu.SemaphoreType.DMA((2,)),
         ],
         compiler_params=PARAMS,
         cost_estimate=flops(8 * own * own * width),
         name="count",
     )(me, features, outgoing[0], neighbours.T, counts_rows)
 
-    adj = pltpu.with_memory_space_constraint(adj, pltpu.HBM)
-    base = pltpu.with_memory_space_constraint(base, pltpu.HBM)
     return pl.pallas_call(
-        last_kernel,
+        functools.partial(last_kernel, peers=n_loc),
         out_shape=jax.ShapeDtypeStruct((own, width), F32),
-        in_specs=[SMEM, HBM, HBM] + [VMEM] * (4 + len(received)),
+        in_specs=[SMEM] + [VMEM] * (5 + len(hub_pieces) + len(received)),
         out_specs=HBM,
         scratch_shapes=[
-            pltpu.VMEM((own, remote), BF),
-            pltpu.VMEM((own, width), F32),
             pltpu.VMEM((own, width), F32),
             pltpu.VMEM((remote, width), BF),
             pltpu.VMEM((remote, width), BF),
-            pltpu.SemaphoreType.DMA((2 * STEPS,)),
             pltpu.SemaphoreType.DMA((STEPS,)),
         ],
         compiler_params=PARAMS,
         cost_estimate=flops(8 * own * own * width),
         name="last",
     )(
-        hub_slot, adj, base, counts_rows, hub_pieces, weight, bias.reshape(1, width), *received
+        hub_slot, adj, base, counts_rows, weight, bias.reshape(1, width), *hub_pieces, *received
     )
 
 

time: 37.1 us -> 45.5 us (1.23)
  waiting for transfers between devices: 0.03 us -> 8.32 us
  starting transfers between devices: 16.3 us -> 19.9 us
  Pallas kernels: 16.7 us -> 14.8 us
  local copies, waits for them, and re-layouts: 3.6 us -> 1.94 us
    ppermute x3 -> x10, waiting for transfers between devices: 0.01 us -> 6.54 us  [the longest x3 5.49 us: on_device(): arrived.append(lax.ppermute(parts[s], 'grp', pairs))]
    ppermute x3 -> x10, starting transfers between devices: 5.71 us -> 11.8 us  [the longest x7 7.32 us: on_device(): hub_pieces.append(lax.ppermute(folded[s], 'loc', pairs))]
    all_to_all x1 -> x0, starting transfers between devices: 3.92 us -> none  [on_device(): lax.all_to_all(group_part, 'loc', split_axis=0, concat_axis=0, tiled=True)]
    pallas_call x2 -> x3, Pallas kernels: 13.9 us -> 12 us  [the longest x1 6.56 us: on_device(): pl.pallas_call(count_kernel, out_shape=[jax.ShapeDtypeStruct((own, remote...]
    ppermute x7, waiting for transfers between devices: 0.02 us -> 1.79 us  [on_device(): received.append(lax.ppermute(outgoing[s], 'loc', pairs))]
    ppermute x7, starting transfers between devices: 6.63 us -> 8.09 us  [on_device(): received.append(lax.ppermute(outgoing[s], 'loc', pairs))]
    unnamed x18, local copies, waits for them, and re-layouts: 2.98 us -> 1.94 us
    reshape x1 -> x0, local copies, waits for them, and re-layouts: 0.63 us -> none  [on_device(): group_part = group_part.reshape(n_loc, owned, width)]
  transfers between devices with their start and end apart: 11 -> 17, of which waited for: 0 -> 7; matrix products, arithmetic and copies ran while one was open for 2% -> 0% of each run, Pallas kernels for 26% -> 18%
where the time goes in v2:
time: 45.5 us; the launch traced here: 45.1 us
  starting transfers between devices  19.9 us (44%)
  Pallas kernels  14.8 us (33%)
  waiting for transfers between devices  8.32 us (18%)
  local copies, waits for them, and re-layouts  1.94 us (4%)
    ppermute x7, starting transfers between devices, on_device(): received.append(lax.ppermute(outgoing[s], 'loc', pairs))  8.09 us
    ppermute x7, starting transfers between devices, on_device(): hub_pieces.append(lax.ppermute(folded[s], 'loc', pairs))  7.32 us
    pallas_call x1, Pallas kernels, on_device(): pl.pallas_call(count_kernel, out_shape=[jax.ShapeDtypeStruct((own, remote...  6.56 us
    ppermute x3, waiting for transfers between devices, on_device(): arrived.append(lax.ppermute(parts[s], 'grp', pairs))  5.49 us
    pallas_call x1, Pallas kernels, on_device(): pl.pallas_call(functools.partial(last_kernel, peers=n_loc), out_shape=jax...  4.81 us
    ppermute x3, starting transfers between devices, on_device(): arrived.append(lax.ppermute(parts[s], 'grp', pairs))  4.45 us
    pallas_call x1, Pallas kernels, on_device(): pl.pallas_call(functools.partial(pick_kernel, peers=n_loc, rows=listed),...  2.02 us
    unnamed x18, local copies, waits for them, and re-layouts  1.94 us
  transfers between devices with their start and end apart: 17, of which 7 were waited for; matrix products, arithmetic and copies ran while one was open for 0% of the time, Pallas kernels for 18%

profile of v2, /device:TPU:0, one launch (start us, length us, event | category | flops | bytes accessed | tf_op | source)
XLA Modules:
  0.0 45.1 jit_solution(5120205418284974993)
XLA Ops:
  0.0 0.1 pad_add_fusion.me
  0.1 1.2 %copy-done = f32[1024,256]{1,0:T(8,128)S(1)} copy-done((f32[1024,256]{1,0:T(8,128)S(1)}, f32[1024,256]{1,0:T(8,128)}, u32[]{:S(2)}) %copy-start) | copy-done | bytes 1048600
  1.3 0.7 %copy-done.5 = s32[8,128]{1,0:T(8,128)S(1)} copy-done((s32[8,128]{1,0:T(8,128)S(1)}, s32[8,128]{1,0:T(8,128)}, u32[]{:S(2)}) %copy-start.5) | copy-done | bytes 4120
  2.0 2.0 %pick.1 = (f32[128,256]{1,0:T(8,128)S(1)}, f32[128,256]{1,0:T(8,128)S(1)}, f32[128,256]{1,0:T(8,128)S(1)}, f32[128,256]{1,0:T(8,128)S(1)}, f32[128,256]{1,0:T(8,...) custom-call(s32[2]{0:T(128)S(1)} %pad_add_fusion.me, f32[1024,256]{1,0:T(8,128)S(1)} %copy-done, ...), custom_call_target="tpu_custom_call" | custom-call | flops 1073741824 | bytes 1048576 | tf_op jit(solution)/shard_map/pick/pallas_call | solution.py:190
  4.0 0.6 %collective-permute-start.10 = (f32[128,256]{1,0:T(8,128)S(1)}, f32[128,256]{1,0:T(8,128)S(1)}, u32[]{:S(2)}, u32[]{:S(2)}) collective-permute-start(f32[128,256]{1,0:T(8,128)S(1)} %get-tuple-element.42), channel_id=1, source_target_pairs={{0,1},{1,0},{2,3},{3,2},{4,5},{5,4},{6,7},{7,6},{8,9},{9,8},{10,11... | collective-permute-start | bytes 393224 | tf_op jit(solution)/shard_map/ppermute | solution.py:203
  4.6 2.6 %collective-permute-start.11 = (f32[128,256]{1,0:T(8,128)S(1)}, f32[128,256]{1,0:T(8,128)S(1)}, u32[]{:S(2)}, u32[]{:S(2)}) collective-permute-start(f32[128,256]{1,0:T(8,128)S(1)} %get-tuple-element.43), channel_id=1, source_target_pairs={{0,2},{1,3},{2,0},{3,1},{4,6},{5,7},{6,4},{7,5},{8,10},{9,11},{10,... | collective-permute-start | bytes 393224 | tf_op jit(solution)/shard_map/ppermute | solution.py:203
  7.1 0.8 %hub.2 = (f32[32,256]{1,0:T(8,128)S(1)}, f32[32,256]{1,0:T(8,128)S(1)}, f32[32,256]{1,0:T(8,128)S(1)}, f32[32,256]{1,0:T(8,128)S(1)}) custom-call(s32[2]{0:T(128)S(1)} %pad_add_fusion.me, f32[1024,256]{1,0:T(8,128)S(1)} %copy-done, bf16[128,1024]{1,0:T(8,128)(2,1)S(1)} %copy-done.2), custom_call_target="tpu_custom_call" | custom-call | flops 67108864 | bytes 1048576 | tf_op jit(solution)/shard_map/hub/pallas_call | solution.py:206
  7.9 1.6 %collective-permute-start = (f32[32,256]{1,0:T(8,128)S(1)}, f32[32,256]{1,0:T(8,128)S(1)}, u32[]{:S(2)}, u32[]{:S(2)}) collective-permute-start(f32[32,256]{1,0:T(8,128)S(1)} %get-tuple-element.31), channel_id=1, source_target_pairs={{0,8},{8,0},{16,24},{24,16},{1,9},{9,1},{17,25},{25,17},{2,10},{10... | collective-permute-start | bytes 98312 | tf_op jit(solution)/shard_map/ppermute | solution.py:219
  9.6 2.6 %collective-permute-start.1 = (f32[32,256]{1,0:T(8,128)S(1)}, f32[32,256]{1,0:T(8,128)S(1)}, u32[]{:S(2)}, u32[]{:S(2)}) collective-permute-start(f32[32,256]{1,0:T(8,128)S(1)} %get-tuple-element.32), channel_id=1, source_target_pairs={{0,16},{8,24},{16,0},{24,8},{1,17},{9,25},{17,1},{25,9},{2,18},{10... | collective-permute-start | bytes 98312 | tf_op jit(solution)/shard_map/ppermute | solution.py:219
  12.2 0.2 collective-permute-start.2
  12.4 2.6 %collective-permute-done.1.refs_2_ = f32[32,256]{1,0:T(8,128)S(1)} collective-permute-done((f32[32,256]{1,0:T(8,128)S(1)}, f32[32,256]{1,0:T(8,128)S(1)}, u32[]{:S(2)}, u32[]{:S(2)}) %collective-permute-start.1) | collective-permute-done | bytes 32800 | tf_op jit(solution)/shard_map/ppermute | solution.py:219
  15.0 2.9 %collective-permute-done.2.refs_3_ = f32[32,256]{1,0:T(8,128)S(1)} collective-permute-done((f32[32,256]{1,0:T(8,128)S(1)}, f32[32,256]{1,0:T(8,128)S(1)}, u32[]{:S(2)}, u32[]{:S(2)}) %collective-permute-start.2) | collective-permute-done | bytes 32800 | tf_op jit(solution)/shard_map/ppermute | solution.py:219
  17.9 0.6 %fold.1 = (f32[4,256]{1,0:T(4,128)S(1)}, f32[4,256]{1,0:T(4,128)S(1)}, f32[4,256]{1,0:T(4,128)S(1)}, f32[4,256]{1,0:T(4,128)S(1)}, f32[4,256]{1,0:T(4,128)S(1)},...) custom-call(s32[2]{0:T(128)S(1)} %pad_add_fusion.me, f32[32,256]{1,0:T(8,128)S(1)} %get-tuple-element.30.refs_0_, ...), custom_call_target="tpu_custom_call" | custom-call | tf_op jit(solution)/shard_map/fold/pallas_call | solution.py:220
  18.5 0.1 collective-permute-start.3
  18.6 0.6 %collective-permute-start.4 = (f32[4,256]{1,0:T(4,128)S(1)}, f32[4,256]{1,0:T(4,128)S(1)}, u32[]{:S(2)}, u32[]{:S(2)}) collective-permute-start(f32[4,256]{1,0:T(4,128)S(1)} %get-tuple-element.36), channel_id=1, source_target_pairs={{0,2},{1,3},{2,0},{3,1},{4,6},{5,7},{6,4},{7,5},{8,10},{9,11},{10,... | collective-permute-start | bytes 12296 | tf_op jit(solution)/shard_map/ppermute | solution.py:232
  19.2 1.2 %collective-permute-start.5 = (f32[4,256]{1,0:T(4,128)S(1)}, f32[4,256]{1,0:T(4,128)S(1)}, u32[]{:S(2)}, u32[]{:S(2)}) collective-permute-start(f32[4,256]{1,0:T(4,128)S(1)} %get-tuple-element.37), channel_id=1, source_target_pairs={{0,3},{1,2},{2,1},{3,0},{4,7},{5,6},{6,5},{7,4},{8,11},{9,10},{10,... | collective-permute-start | bytes 12296 | tf_op jit(solution)/shard_map/ppermute | solution.py:232
  20.4 1.5 %collective-permute-start.6 = (f32[4,256]{1,0:T(4,128)S(1)}, f32[4,256]{1,0:T(4,128)S(1)}, u32[]{:S(2)}, u32[]{:S(2)}) collective-permute-start(f32[4,256]{1,0:T(4,128)S(1)} %get-tuple-element.38), channel_id=1, source_target_pairs={{0,4},{1,5},{2,6},{3,7},{4,0},{5,1},{6,2},{7,3},{8,12},{9,13},{10,... | collective-permute-start | bytes 12296 | tf_op jit(solution)/shard_map/ppermute | solution.py:232
  21.9 0.3 collective-permute-done.4.refs_2_
  22.3 0.4 collective-permute-start.7
  22.7 2.0 %collective-permute-start.8 = (f32[4,256]{1,0:T(4,128)S(1)}, f32[4,256]{1,0:T(4,128)S(1)}, u32[]{:S(2)}, u32[]{:S(2)}) collective-permute-start(f32[4,256]{1,0:T(4,128)S(1)} %get-tuple-element.40), channel_id=1, source_target_pairs={{0,6},{1,7},{2,4},{3,5},{4,2},{5,3},{6,0},{7,1},{8,14},{9,15},{10,... | collective-permute-start | bytes 12296 | tf_op jit(solution)/shard_map/ppermute | solution.py:232
  24.7 1.5 %collective-permute-start.9 = (f32[4,256]{1,0:T(4,128)S(1)}, f32[4,256]{1,0:T(4,128)S(1)}, u32[]{:S(2)}, u32[]{:S(2)}) collective-permute-start(f32[4,256]{1,0:T(4,128)S(1)} %get-tuple-element.41), channel_id=1, source_target_pairs={{0,7},{1,6},{2,5},{3,4},{4,3},{5,2},{6,1},{7,0},{8,15},{9,14},{10,... | collective-permute-start | bytes 12296 | tf_op jit(solution)/shard_map/ppermute | solution.py:232
  26.1 0.6 %collective-permute-start.12 = (f32[128,256]{1,0:T(8,128)S(1)}, f32[128,256]{1,0:T(8,128)S(1)}, u32[]{:S(2)}, u32[]{:S(2)}) collective-permute-start(f32[128,256]{1,0:T(8,128)S(1)} %get-tuple-element.44), channel_id=1, source_target_pairs={{0,3},{1,2},{2,1},{3,0},{4,7},{5,6},{6,5},{7,4},{8,11},{9,10},{10,... | collective-permute-start | bytes 393224 | tf_op jit(solution)/shard_map/ppermute | solution.py:203
  26.7 0.4 collective-permute-done.8.refs_6_
  27.2 1.1 %collective-permute-start.13 = (f32[128,256]{1,0:T(8,128)S(1)}, f32[128,256]{1,0:T(8,128)S(1)}, u32[]{:S(2)}, u32[]{:S(2)}) collective-permute-start(f32[128,256]{1,0:T(8,128)S(1)} %get-tuple-element.45), channel_id=1, source_target_pairs={{0,4},{1,5},{2,6},{3,7},{4,0},{5,1},{6,2},{7,3},{8,12},{9,13},{10,... | collective-permute-start | bytes 393224 | tf_op jit(solution)/shard_map/ppermute | solution.py:203
  28.3 0.3 collective-permute-done.9.refs_7_
  28.6 0.6 %collective-permute-start.14 = (f32[128,256]{1,0:T(8,128)S(1)}, f32[128,256]{1,0:T(8,128)S(1)}, u32[]{:S(2)}, u32[]{:S(2)}) collective-permute-start(f32[128,256]{1,0:T(8,128)S(1)} %get-tuple-element.46), channel_id=1, source_target_pairs={{0,5},{1,4},{2,7},{3,6},{4,1},{5,0},{6,3},{7,2},{8,13},{9,12},{10,... | collective-permute-start | bytes 393224 | tf_op jit(solution)/shard_map/ppermute | solution.py:203
  29.2 1.4 %collective-permute-start.15 = (f32[128,256]{1,0:T(8,128)S(1)}, f32[128,256]{1,0:T(8,128)S(1)}, u32[]{:S(2)}, u32[]{:S(2)}) collective-permute-start(f32[128,256]{1,0:T(8,128)S(1)} %get-tuple-element.47), channel_id=1, source_target_pairs={{0,6},{1,7},{2,4},{3,5},{4,2},{5,3},{6,0},{7,1},{8,14},{9,15},{10,... | collective-permute-start | bytes 393224 | tf_op jit(solution)/shard_map/ppermute | solution.py:203
  30.6 1.3 %collective-permute-start.16 = (f32[128,256]{1,0:T(8,128)S(1)}, f32[128,256]{1,0:T(8,128)S(1)}, u32[]{:S(2)}, u32[]{:S(2)}) collective-permute-start(f32[128,256]{1,0:T(8,128)S(1)} %get-tuple-element.48), channel_id=1, source_target_pairs={{0,7},{1,6},{2,5},{3,4},{4,3},{5,2},{6,1},{7,0},{8,15},{9,14},{10,... | collective-permute-start | bytes 393224 | tf_op jit(solution)/shard_map/ppermute | solution.py:203
  31.9 6.6 %count.1 = (bf16[1024,896]{1,0:T(8,128)(2,1)S(1)}, f32[1024,256]{1,0:T(8,128)S(1)}) custom-call(s32[2]{0:T(128)S(1)} %pad_add_fusion.me, f32[1024,256]{1,0:T(8,128)S(1)} %copy-done.1, f32[128,256]{1,0:T(8,128)S(1)} %get-tuple-element.27.mine, s32[16,1024]{1,0:T(8,128)S(1)} %bitcast.5, s32[8,128]{1,0:T(8,128)S(1)} %bitcast.6), custom_call_target="tpu_custom_call" | custom-call | flops 2147483648 | bytes 1048576 | tf_op jit(solution)/shard_map/count/pallas_call | solution.py:238
  38.5 0.7 %collective-permute-done.13.refs_11_ = f32[128,256]{1,0:T(8,128)S(1)} collective-permute-done((f32[128,256]{1,0:T(8,128)S(1)}, f32[128,256]{1,0:T(8,128)S(1)}, u32[]{:S(2)}, u32[]{:S(2)}) %collective-permute-start.13) | collective-permute-done | bytes 131104 | tf_op jit(solution)/shard_map/ppermute | solution.py:203
  39.2 1.1 %collective-permute-done.14.refs_12_ = f32[128,256]{1,0:T(8,128)S(1)} collective-permute-done((f32[128,256]{1,0:T(8,128)S(1)}, f32[128,256]{1,0:T(8,128)S(1)}, u32[]{:S(2)}, u32[]{:S(2)}) %collective-permute-start.14) | collective-permute-done | bytes 131104 | tf_op jit(solution)/shard_map/ppermute | solution.py:203
  40.3 4.8 %last.1 = f32[1024,256]{1,0:T(8,128)} custom-call(s32[4]{0:T(128)S(1)} %copy-done.8, bf16[1024,896]{1,0:T(8,128)(2,1)S(1)} %get-tuple-element.28.adj, f32[1024,256]{1,0:T(8,128)S(1)} %get-tuple-element.29.base, s32[8,128]{1,0:T(8,128)S(1)} %bitcast.7, f32[256,256]{1,0:T(8,128)S(1)} %copy-done.3, f32[1,256]{1,0:T(1,128)S(1)} %bitcast.8, ...), custom_call_target="tpu_custom_call" | custom-call | flops 2147483648 | bytes 1048576 | tf_op jit(solution)/shard_map/last/pallas_call | solution.py:256
  (26 shorter events, 0.1 us)
Async XLA Ops:
  0.1 1.2 %copy-start = (f32[1024,256]{1,0:T(8,128)S(1)}, f32[1024,256]{1,0:T(8,128)}, u32[]{:S(2)}) copy-start(f32[1024,256]{1,0:T(8,128)} %features.5) | copy-start | bytes 3145732
  1.3 0.7 %copy-start.5 = (s32[8,128]{1,0:T(8,128)S(1)}, s32[8,128]{1,0:T(8,128)}, u32[]{:S(2)}) copy-start(s32[8,128]{1,0:T(8,128)} %halo.1) | copy-start | bytes 12292
  2.0 5.2 %copy-start.2 = (bf16[128,1024]{1,0:T(8,128)(2,1)S(1)}, bf16[128,1024]{1,0:T(8,128)(2,1)}, u32[]{:S(2)}) copy-start(bf16[128,1024]{1,0:T(8,128)(2,1)} %hub.3) | copy-start | bytes 786436
  2.0 29.9 %copy-start.1 = (f32[1024,256]{1,0:T(8,128)S(1)}, f32[1024,256]{1,0:T(8,128)}, u32[]{:S(2)}) copy-start(f32[1024,256]{1,0:T(8,128)} %features.5) | copy-start | bytes 3145732
  2.0 29.9 %copy-start.4 = (s32[1024,16]{0,1:T(8,128)S(1)}, s32[1024,16]{0,1:T(8,128)}, u32[]{:S(2)}) copy-start(s32[1024,16]{0,1:T(8,128)} %param.11) | copy-start | bytes 196612
  2.0 29.9 %copy-start.6 = (s32[1024]{0:T(1024)S(1)}, s32[1024]{0:T(1024)}, u32[]{:S(2)}) copy-start(s32[1024]{0:T(1024)} %param.12) | copy-start | bytes 12292
  4.0 25.2 %collective-permute-start.10 = (f32[128,256]{1,0:T(8,128)S(1)}, f32[128,256]{1,0:T(8,128)S(1)}, u32[]{:S(2)}, u32[]{:S(2)}) collective-permute-start(f32[128,256]{1,0:T(8,128)S(1)} %get-tuple-element.42), channel_id=1, source_target_pairs={{0,1},{1,0},{2,3},{3,2},{4,5},{5,4},{6,7},{7,6},{8,9},{9,8},{10,11... | collective-permute-start | bytes 393224 | tf_op jit(solution)/shard_map/ppermute | solution.py:203
  4.6 26.0 %collective-permute-start.11 = (f32[128,256]{1,0:T(8,128)S(1)}, f32[128,256]{1,0:T(8,128)S(1)}, u32[]{:S(2)}, u32[]{:S(2)}) collective-permute-start(f32[128,256]{1,0:T(8,128)S(1)} %get-tuple-element.43), channel_id=1, source_target_pairs={{0,2},{1,3},{2,0},{3,1},{4,6},{5,7},{6,4},{7,5},{8,10},{9,11},{10,... | collective-permute-start | bytes 393224 | tf_op jit(solution)/shard_map/ppermute | solution.py:203
  7.9 4.5 %collective-permute-start = (f32[32,256]{1,0:T(8,128)S(1)}, f32[32,256]{1,0:T(8,128)S(1)}, u32[]{:S(2)}, u32[]{:S(2)}) collective-permute-start(f32[32,256]{1,0:T(8,128)S(1)} %get-tuple-element.31), channel_id=1, source_target_pairs={{0,8},{8,0},{16,24},{24,16},{1,9},{9,1},{17,25},{25,17},{2,10},{10... | collective-permute-start | bytes 98312 | tf_op jit(solution)/shard_map/ppermute | solution.py:219
  9.6 5.4 %collective-permute-start.1 = (f32[32,256]{1,0:T(8,128)S(1)}, f32[32,256]{1,0:T(8,128)S(1)}, u32[]{:S(2)}, u32[]{:S(2)}) collective-permute-start(f32[32,256]{1,0:T(8,128)S(1)} %get-tuple-element.32), channel_id=1, source_target_pairs={{0,16},{8,24},{16,0},{24,8},{1,17},{9,25},{17,1},{25,9},{2,18},{10... | collective-permute-start | bytes 98312 | tf_op jit(solution)/shard_map/ppermute | solution.py:219
  12.2 5.7 %collective-permute-start.2 = (f32[32,256]{1,0:T(8,128)S(1)}, f32[32,256]{1,0:T(8,128)S(1)}, u32[]{:S(2)}, u32[]{:S(2)}) collective-permute-start(f32[32,256]{1,0:T(8,128)S(1)} %get-tuple-element.33), channel_id=1, source_target_pairs={{0,24},{8,16},{16,8},{24,0},{1,25},{9,17},{17,9},{25,1},{2,26},{10... | collective-permute-start | bytes 98312 | tf_op jit(solution)/shard_map/ppermute | solution.py:219
  18.5 1.9 %collective-permute-start.3 = (f32[4,256]{1,0:T(4,128)S(1)}, f32[4,256]{1,0:T(4,128)S(1)}, u32[]{:S(2)}, u32[]{:S(2)}) collective-permute-start(f32[4,256]{1,0:T(4,128)S(1)} %get-tuple-element.35), channel_id=1, source_target_pairs={{0,1},{1,0},{2,3},{3,2},{4,5},{5,4},{6,7},{7,6},{8,9},{9,8},{10,11... | collective-permute-start | bytes 12296 | tf_op jit(solution)/shard_map/ppermute | solution.py:232
  18.6 3.7 %collective-permute-start.4 = (f32[4,256]{1,0:T(4,128)S(1)}, f32[4,256]{1,0:T(4,128)S(1)}, u32[]{:S(2)}, u32[]{:S(2)}) collective-permute-start(f32[4,256]{1,0:T(4,128)S(1)} %get-tuple-element.36), channel_id=1, source_target_pairs={{0,2},{1,3},{2,0},{3,1},{4,6},{5,7},{6,4},{7,5},{8,10},{9,11},{10,... | collective-permute-start | bytes 12296 | tf_op jit(solution)/shard_map/ppermute | solution.py:232
  19.2 3.5 %collective-permute-start.5 = (f32[4,256]{1,0:T(4,128)S(1)}, f32[4,256]{1,0:T(4,128)S(1)}, u32[]{:S(2)}, u32[]{:S(2)}) collective-permute-start(f32[4,256]{1,0:T(4,128)S(1)} %get-tuple-element.37), channel_id=1, source_target_pairs={{0,3},{1,2},{2,1},{3,0},{4,7},{5,6},{6,5},{7,4},{8,11},{9,10},{10,... | collective-permute-start | bytes 12296 | tf_op jit(solution)/shard_map/ppermute | solution.py:232
  20.4 4.2 %collective-permute-start.6 = (f32[4,256]{1,0:T(4,128)S(1)}, f32[4,256]{1,0:T(4,128)S(1)}, u32[]{:S(2)}, u32[]{:S(2)}) collective-permute-start(f32[4,256]{1,0:T(4,128)S(1)} %get-tuple-element.38), channel_id=1, source_target_pairs={{0,4},{1,5},{2,6},{3,7},{4,0},{5,1},{6,2},{7,3},{8,12},{9,13},{10,... | collective-permute-start | bytes 12296 | tf_op jit(solution)/shard_map/ppermute | solution.py:232
  22.3 3.9 %collective-permute-start.7 = (f32[4,256]{1,0:T(4,128)S(1)}, f32[4,256]{1,0:T(4,128)S(1)}, u32[]{:S(2)}, u32[]{:S(2)}) collective-permute-start(f32[4,256]{1,0:T(4,128)S(1)} %get-tuple-element.39), channel_id=1, source_target_pairs={{0,5},{1,4},{2,7},{3,6},{4,1},{5,0},{6,3},{7,2},{8,13},{9,12},{10,... | collective-permute-start | bytes 12296 | tf_op jit(solution)/shard_map/ppermute | solution.py:232
  22.7 4.5 %collective-permute-start.8 = (f32[4,256]{1,0:T(4,128)S(1)}, f32[4,256]{1,0:T(4,128)S(1)}, u32[]{:S(2)}, u32[]{:S(2)}) collective-permute-start(f32[4,256]{1,0:T(4,128)S(1)} %get-tuple-element.40), channel_id=1, source_target_pairs={{0,6},{1,7},{2,4},{3,5},{4,2},{5,3},{6,0},{7,1},{8,14},{9,15},{10,... | collective-permute-start | bytes 12296 | tf_op jit(solution)/shard_map/ppermute | solution.py:232
  24.7 3.9 %collective-permute-start.9 = (f32[4,256]{1,0:T(4,128)S(1)}, f32[4,256]{1,0:T(4,128)S(1)}, u32[]{:S(2)}, u32[]{:S(2)}) collective-permute-start(f32[4,256]{1,0:T(4,128)S(1)} %get-tuple-element.41), channel_id=1, source_target_pairs={{0,7},{1,6},{2,5},{3,4},{4,3},{5,2},{6,1},{7,0},{8,15},{9,14},{10,... | collective-permute-start | bytes 12296 | tf_op jit(solution)/shard_map/ppermute | solution.py:232
  26.1 12.3 %collective-permute-start.12 = (f32[128,256]{1,0:T(8,128)S(1)}, f32[128,256]{1,0:T(8,128)S(1)}, u32[]{:S(2)}, u32[]{:S(2)}) collective-permute-start(f32[128,256]{1,0:T(8,128)S(1)} %get-tuple-element.44), channel_id=1, source_target_pairs={{0,3},{1,2},{2,1},{3,0},{4,7},{5,6},{6,5},{7,4},{8,11},{9,10},{10,... | collective-permute-start | bytes 393224 | tf_op jit(solution)/shard_map/ppermute | solution.py:203
  27.2 12.0 %collective-permute-start.13 = (f32[128,256]{1,0:T(8,128)S(1)}, f32[128,256]{1,0:T(8,128)S(1)}, u32[]{:S(2)}, u32[]{:S(2)}) collective-permute-start(f32[128,256]{1,0:T(8,128)S(1)} %get-tuple-element.45), channel_id=1, source_target_pairs={{0,4},{1,5},{2,6},{3,7},{4,0},{5,1},{6,2},{7,3},{8,12},{9,13},{10,... | collective-permute-start | bytes 393224 | tf_op jit(solution)/shard_map/ppermute | solution.py:203
  28.6 11.7 %collective-permute-start.14 = (f32[128,256]{1,0:T(8,128)S(1)}, f32[128,256]{1,0:T(8,128)S(1)}, u32[]{:S(2)}, u32[]{:S(2)}) collective-permute-start(f32[128,256]{1,0:T(8,128)S(1)} %get-tuple-element.46), channel_id=1, source_target_pairs={{0,5},{1,4},{2,7},{3,6},{4,1},{5,0},{6,3},{7,2},{8,13},{9,12},{10,... | collective-permute-start | bytes 393224 | tf_op jit(solution)/shard_map/ppermute | solution.py:203
  29.2 11.0 %collective-permute-start.15 = (f32[128,256]{1,0:T(8,128)S(1)}, f32[128,256]{1,0:T(8,128)S(1)}, u32[]{:S(2)}, u32[]{:S(2)}) collective-permute-start(f32[128,256]{1,0:T(8,128)S(1)} %get-tuple-element.47), channel_id=1, source_target_pairs={{0,6},{1,7},{2,4},{3,5},{4,2},{5,3},{6,0},{7,1},{8,14},{9,15},{10,... | collective-permute-start | bytes 393224 | tf_op jit(solution)/shard_map/ppermute | solution.py:203
  30.6 9.7 %collective-permute-start.16 = (f32[128,256]{1,0:T(8,128)S(1)}, f32[128,256]{1,0:T(8,128)S(1)}, u32[]{:S(2)}, u32[]{:S(2)}) collective-permute-start(f32[128,256]{1,0:T(8,128)S(1)} %get-tuple-element.48), channel_id=1, source_target_pairs={{0,7},{1,6},{2,5},{3,4},{4,3},{5,2},{6,1},{7,0},{8,15},{9,14},{10,... | collective-permute-start | bytes 393224 | tf_op jit(solution)/shard_map/ppermute | solution.py:203
  31.9 8.4 %copy-start.3 = (f32[256,256]{1,0:T(8,128)S(1)}, f32[256,256]{1,0:T(8,128)}, u32[]{:S(2)}) copy-start(f32[256,256]{1,0:T(8,128)} %weight.1) | copy-start | bytes 786436
  31.9 8.4 %copy-start.7 = (f32[256]{0:T(256)S(1)}, f32[256]{0:T(256)}, u32[]{:S(2)}) copy-start(f32[256]{0:T(256)} %param.15) | copy-start | bytes 3076
  31.9 8.4 %copy-start.8 = (s32[4]{0:T(128)S(1)}, s32[4]{0:T(128)}, u32[]{:S(2)}) copy-start(s32[4]{0:T(128)} %slot.1) | copy-start | bytes 52

commit v3 on v2

--- a/solution.py
+++ b/solution.py
@@ -11,7 +11,6 @@
 BF = jnp.bfloat16
 F32 = jnp.float32
 LANES = 128
-STEPS = 4
 GROUP = 16
 
 
@@ -66,10 +65,8 @@
     return 1.0 / counts[...].astype(F32).T
 
 
-def count_kernel(me, features, mine, names, counts, far_s, base, code_s, low_s, near_s):
-    own, _ = features.shape
-    degree = names.shape[0]
-    listed = mine.shape[0]
+def count_kernel(me, names, counts, near_s, far_s, code_s, low_s, *, listed):
+    degree, own = names.shape
     tiles = own // LANES
     span = GROUP * degree
     each = LANES // GROUP
@@ -125,41 +122,38 @@
         return 0
 
     lax.fori_loop(0, tiles, build, 0)
+
+
+def near_kernel(near, features, mine, counts, base):
     hi, lo = split(jnp.concatenate([features[...], mine[...]], axis=0))
     inv = inverse_counts(counts)
-    for j in range(tiles):
+    for j in range(near.shape[0] // LANES):
         cut = slice(j * LANES, (j + 1) * LANES)
-        a = near_s[cut, :]
+        a = near[cut, :]
         base[cut, :] = features[cut, :] + (mm(a, hi) + mm(a, lo)) * inv[:, j : j + 1]
 
 
 def last_kernel(slot, adj, base, counts, weight, bias, *refs, peers):
-    hubs, pieces, (out, out_s, rhi, rlo, ends) = refs[:peers], refs[peers:-5], refs[-5:]
-    size = pieces[0].shape[0]
-    rows = adj.shape[0] // STEPS
-    cuts = [pl.ds(n * rows, rows) for n in range(STEPS)]
-    for n, piece in enumerate(pieces):
-        cut = slice(n * size, (n + 1) * size)
-        rhi[cut, :], rlo[cut, :] = split(piece[...])
-    whi, wlo = split(weight[...])
+    hubs, pieces, (out, comb, out_s, ends) = refs[:peers], refs[peers:-4], refs[-4:]
+    hi, lo = split(jnp.concatenate([piece[...] for piece in pieces], axis=0))
     inv = inverse_counts(counts)
+    cuts = [slice(j * LANES, (j + 1) * LANES) for j in range(adj.shape[0] // LANES)]
+    for j, cut in enumerate(cuts):
+        a = adj[cut, :]
+        comb[cut, :] = base[cut, :] + (mm(a, hi) + mm(a, lo)) * inv[:, j : j + 1]
     sums = hubs[0][...]
     for hub in hubs[1:]:
         sums = sums + hub[...]
-    per = rows // LANES
+    for i in range(sums.shape[0]):
+        at = slot[i]
+        comb[pl.ds(at, 1), :] = comb[pl.ds(at, 1), :] + sums[i : i + 1]
+    whi, wlo = split(weight[...])
     stores = []
-    for n, cut in enumerate(cuts):
-        a = adj[cut, :]
-        summed = mm(a, rhi[...]) + mm(a, rlo[...])
-        scale = jnp.concatenate([inv[:, n * per + j : n * per + j + 1] for j in range(per)], axis=0)
-        comb = base[cut, :] + summed * scale
-        row = lax.broadcasted_iota(jnp.int32, (rows, 1), 0) + n * rows
-        for i in range(sums.shape[0]):
-            comb = comb + jnp.where(row == slot[i], sums[i : i + 1], 0.0)
-        chi, clo = split(comb)
+    for j, cut in enumerate(cuts):
+        chi, clo = split(comb[cut, :])
         made = mm(chi, whi) + (mm(chi, wlo) + mm(clo, whi)) + bias[...]
         out_s[cut, :] = jnp.maximum(made, 0.0)
-        store = pltpu.make_async_copy(out_s.at[cut], out.at[cut], ends.at[n])
+        store = pltpu.make_async_copy(out_s.at[cut], out.at[cut], ends.at[j])
         store.start()
         stores.append(store)
     for store in stores:
@@ -235,23 +229,28 @@
     tiles = own // LANES
     counts_rows = counts.reshape(tiles, LANES)
     line = (tiles, LANES * degree)
-    adj, base = pl.pallas_call(
-        count_kernel,
+    near, adj = pl.pallas_call(
+        functools.partial(count_kernel, listed=listed),
         out_shape=[
+            jax.ShapeDtypeStruct((own, own + listed), BF),
             jax.ShapeDtypeStruct((own, remote), BF),
-            jax.ShapeDtypeStruct((own, width), F32),
         ],
-        in_specs=[SMEM] + [VMEM] * 4,
+        in_specs=[SMEM] + [VMEM] * 2,
         out_specs=[VMEM] * 2,
-        scratch_shapes=[
-            pltpu.VMEM(line, F32),
-            pltpu.VMEM(line, F32),
-            pltpu.VMEM((own, own + listed), BF),
-        ],
-        compiler_params=PARAMS,
-        cost_estimate=flops(8 * own * own * width),
+        scratch_shapes=[pltpu.VMEM(line, F32)] * 2,
+        compiler_params=PARAMS,
+        cost_estimate=flops(4 * own * own * width),
         name="count",
-    )(me, features, outgoing[0], neighbours.T, counts_rows)
+    )(me, neighbours.T, counts_rows)
+    base = pl.pallas_call(
+        near_kernel,
+        out_shape=jax.ShapeDtypeStruct((own, width), F32),
+        in_specs=[VMEM] * 4,
+        out_specs=VMEM,
+        compiler_params=PARAMS,
+        cost_estimate=flops(4 * own * own * width),
+        name="near",
+    )(near, features, outgoing[0], counts_rows)
 
     return pl.pallas_call(
         functools.partial(last_kernel, peers=n_loc),
@@ -260,9 +259,8 @@
         out_specs=HBM,
         scratch_shapes=[
             pltpu.VMEM((own, width), F32),
-            pltpu.VMEM((remote, width), BF),
-            pltpu.VMEM((remote, width), BF),
-            pltpu.SemaphoreType.DMA((STEPS,)),
+            pltpu.VMEM((own, width), F32),
+            pltpu.SemaphoreType.DMA((tiles,)),
         ],
         compiler_params=PARAMS,
         cost_estimate=flops(8 * own * own * width),

time: 45.5 us -> 43.9 us (0.965)
  Pallas kernels: 14.8 us -> 13.2 us
    pallas_call x1, Pallas kernels: 4.81 us -> 3.27 us  [on_device(): pl.pallas_call(functools.partial(last_kernel, peers=n_loc), out_shape=jax...]
    pallas_call x1 -> x2, Pallas kernels: 6.56 us -> 6.56 us  [the longest x1 4.91 us: on_device(): pl.pallas_call(functools.partial(count_kernel, listed=listed), out_shape=...]
where the time goes in v3:
time: 43.9 us; the launch traced here: 43.6 us
  starting transfers between devices  19.9 us (45%)
  Pallas kernels  13.2 us (30%)
  waiting for transfers between devices  8.3 us (19%)
  local copies, waits for them, and re-layouts  1.95 us (4%)
    ppermute x7, starting transfers between devices, on_device(): received.append(lax.ppermute(outgoing[s], 'loc', pairs))  8.09 us
    ppermute x7, starting transfers between devices, on_device(): hub_pieces.append(lax.ppermute(folded[s], 'loc', pairs))  7.32 us
    ppermute x3, waiting for transfers between devices, on_device(): arrived.append(lax.ppermute(parts[s], 'grp', pairs))  5.49 us
    pallas_call x1, Pallas kernels, on_device(): pl.pallas_call(functools.partial(count_kernel, listed=listed), out_shape=...  4.91 us
    ppermute x3, starting transfers between devices, on_device(): arrived.append(lax.ppermute(parts[s], 'grp', pairs))  4.45 us
    pallas_call x1, Pallas kernels, on_device(): pl.pallas_call(functools.partial(last_kernel, peers=n_loc), out_shape=jax...  3.27 us
    pallas_call x1, Pallas kernels, on_device(): pl.pallas_call(functools.partial(pick_kernel, peers=n_loc, rows=listed),...  2.02 us
    unnamed x18, local copies, waits for them, and re-layouts  1.95 us
  transfers between devices with their start and end apart: 17, of which 7 were waited for; matrix products, arithmetic and copies ran while one was open for 0% of the time, Pallas kernels for 18%

profile of v3, /device:TPU:0, one launch (start us, length us, event | category | flops | bytes accessed | tf_op | source)
XLA Modules:
  0.0 43.6 jit_solution(17810855915885779974)
XLA Ops:
  0.0 0.1 pad_add_fusion.me
  0.1 1.2 %copy-done = f32[1024,256]{1,0:T(8,128)S(1)} copy-done((f32[1024,256]{1,0:T(8,128)S(1)}, f32[1024,256]{1,0:T(8,128)}, u32[]{:S(2)}) %copy-start) | copy-done | bytes 1048600
  1.3 0.7 %copy-done.6 = s32[8,128]{1,0:T(8,128)S(1)} copy-done((s32[8,128]{1,0:T(8,128)S(1)}, s32[8,128]{1,0:T(8,128)}, u32[]{:S(2)}) %copy-start.6) | copy-done | bytes 4120
  2.0 2.0 %pick.1 = (f32[128,256]{1,0:T(8,128)S(1)}, f32[128,256]{1,0:T(8,128)S(1)}, f32[128,256]{1,0:T(8,128)S(1)}, f32[128,256]{1,0:T(8,128)S(1)}, f32[128,256]{1,0:T(8,...) custom-call(s32[2]{0:T(128)S(1)} %pad_add_fusion.me, f32[1024,256]{1,0:T(8,128)S(1)} %copy-done, ...), custom_call_target="tpu_custom_call" | custom-call | flops 1073741824 | bytes 1048576 | tf_op jit(solution)/shard_map/pick/pallas_call | solution.py:184
  4.0 0.6 %collective-permute-start.10 = (f32[128,256]{1,0:T(8,128)S(1)}, f32[128,256]{1,0:T(8,128)S(1)}, u32[]{:S(2)}, u32[]{:S(2)}) collective-permute-start(f32[128,256]{1,0:T(8,128)S(1)} %get-tuple-element.42), channel_id=1, source_target_pairs={{0,1},{1,0},{2,3},{3,2},{4,5},{5,4},{6,7},{7,6},{8,9},{9,8},{10,11... | collective-permute-start | bytes 393224 | tf_op jit(solution)/shard_map/ppermute | solution.py:197
  4.6 2.6 %collective-permute-start.11 = (f32[128,256]{1,0:T(8,128)S(1)}, f32[128,256]{1,0:T(8,128)S(1)}, u32[]{:S(2)}, u32[]{:S(2)}) collective-permute-start(f32[128,256]{1,0:T(8,128)S(1)} %get-tuple-element.43), channel_id=1, source_target_pairs={{0,2},{1,3},{2,0},{3,1},{4,6},{5,7},{6,4},{7,5},{8,10},{9,11},{10,... | collective-permute-start | bytes 393224 | tf_op jit(solution)/shard_map/ppermute | solution.py:197
  7.1 0.8 %hub.2 = (f32[32,256]{1,0:T(8,128)S(1)}, f32[32,256]{1,0:T(8,128)S(1)}, f32[32,256]{1,0:T(8,128)S(1)}, f32[32,256]{1,0:T(8,128)S(1)}) custom-call(s32[2]{0:T(128)S(1)} %pad_add_fusion.me, f32[1024,256]{1,0:T(8,128)S(1)} %copy-done, bf16[128,1024]{1,0:T(8,128)(2,1)S(1)} %copy-done.2), custom_call_target="tpu_custom_call" | custom-call | flops 67108864 | bytes 1048576 | tf_op jit(solution)/shard_map/hub/pallas_call | solution.py:200
  7.9 1.6 %collective-permute-start = (f32[32,256]{1,0:T(8,128)S(1)}, f32[32,256]{1,0:T(8,128)S(1)}, u32[]{:S(2)}, u32[]{:S(2)}) collective-permute-start(f32[32,256]{1,0:T(8,128)S(1)} %get-tuple-element.31), channel_id=1, source_target_pairs={{0,8},{8,0},{16,24},{24,16},{1,9},{9,1},{17,25},{25,17},{2,10},{10... | collective-permute-start | bytes 98312 | tf_op jit(solution)/shard_map/ppermute | solution.py:213
  9.6 2.6 %collective-permute-start.1 = (f32[32,256]{1,0:T(8,128)S(1)}, f32[32,256]{1,0:T(8,128)S(1)}, u32[]{:S(2)}, u32[]{:S(2)}) collective-permute-start(f32[32,256]{1,0:T(8,128)S(1)} %get-tuple-element.32), channel_id=1, source_target_pairs={{0,16},{8,24},{16,0},{24,8},{1,17},{9,25},{17,1},{25,9},{2,18},{10... | collective-permute-start | bytes 98312 | tf_op jit(solution)/shard_map/ppermute | solution.py:213
  12.2 0.2 collective-permute-start.2
  12.4 2.6 %collective-permute-done.1.refs_2_ = f32[32,256]{1,0:T(8,128)S(1)} collective-permute-done((f32[32,256]{1,0:T(8,128)S(1)}, f32[32,256]{1,0:T(8,128)S(1)}, u32[]{:S(2)}, u32[]{:S(2)}) %collective-permute-start.1) | collective-permute-done | bytes 32800 | tf_op jit(solution)/shard_map/ppermute | solution.py:213
  15.0 2.9 %collective-permute-done.2.refs_3_ = f32[32,256]{1,0:T(8,128)S(1)} collective-permute-done((f32[32,256]{1,0:T(8,128)S(1)}, f32[32,256]{1,0:T(8,128)S(1)}, u32[]{:S(2)}, u32[]{:S(2)}) %collective-permute-start.2) | collective-permute-done | bytes 32800 | tf_op jit(solution)/shard_map/ppermute | solution.py:213
  17.9 0.6 %fold.1 = (f32[4,256]{1,0:T(4,128)S(1)}, f32[4,256]{1,0:T(4,128)S(1)}, f32[4,256]{1,0:T(4,128)S(1)}, f32[4,256]{1,0:T(4,128)S(1)}, f32[4,256]{1,0:T(4,128)S(1)},...) custom-call(s32[2]{0:T(128)S(1)} %pad_add_fusion.me, f32[32,256]{1,0:T(8,128)S(1)} %get-tuple-element.30.refs_0_, ...), custom_call_target="tpu_custom_call" | custom-call | tf_op jit(solution)/shard_map/fold/pallas_call | solution.py:214
  18.6 0.6 %collective-permute-start.4 = (f32[4,256]{1,0:T(4,128)S(1)}, f32[4,256]{1,0:T(4,128)S(1)}, u32[]{:S(2)}, u32[]{:S(2)}) collective-permute-start(f32[4,256]{1,0:T(4,128)S(1)} %get-tuple-element.36), channel_id=1, source_target_pairs={{0,2},{1,3},{2,0},{3,1},{4,6},{5,7},{6,4},{7,5},{8,10},{9,11},{10,... | collective-permute-start | bytes 12296 | tf_op jit(solution)/shard_map/ppermute | solution.py:226
  19.2 1.2 %collective-permute-start.5 = (f32[4,256]{1,0:T(4,128)S(1)}, f32[4,256]{1,0:T(4,128)S(1)}, u32[]{:S(2)}, u32[]{:S(2)}) collective-permute-start(f32[4,256]{1,0:T(4,128)S(1)} %get-tuple-element.37), channel_id=1, source_target_pairs={{0,3},{1,2},{2,1},{3,0},{4,7},{5,6},{6,5},{7,4},{8,11},{9,10},{10,... | collective-permute-start | bytes 12296 | tf_op jit(solution)/shard_map/ppermute | solution.py:226
  20.4 1.5 %collective-permute-start.6 = (f32[4,256]{1,0:T(4,128)S(1)}, f32[4,256]{1,0:T(4,128)S(1)}, u32[]{:S(2)}, u32[]{:S(2)}) collective-permute-start(f32[4,256]{1,0:T(4,128)S(1)} %get-tuple-element.38), channel_id=1, source_target_pairs={{0,4},{1,5},{2,6},{3,7},{4,0},{5,1},{6,2},{7,3},{8,12},{9,13},{10,... | collective-permute-start | bytes 12296 | tf_op jit(solution)/shard_map/ppermute | solution.py:226
  21.9 0.3 collective-permute-done.4.refs_2_
  22.3 0.4 collective-permute-start.7
  22.7 2.0 %collective-permute-start.8 = (f32[4,256]{1,0:T(4,128)S(1)}, f32[4,256]{1,0:T(4,128)S(1)}, u32[]{:S(2)}, u32[]{:S(2)}) collective-permute-start(f32[4,256]{1,0:T(4,128)S(1)} %get-tuple-element.40), channel_id=1, source_target_pairs={{0,6},{1,7},{2,4},{3,5},{4,2},{5,3},{6,0},{7,1},{8,14},{9,15},{10,... | collective-permute-start | bytes 12296 | tf_op jit(solution)/shard_map/ppermute | solution.py:226
  24.7 1.5 %collective-permute-start.9 = (f32[4,256]{1,0:T(4,128)S(1)}, f32[4,256]{1,0:T(4,128)S(1)}, u32[]{:S(2)}, u32[]{:S(2)}) collective-permute-start(f32[4,256]{1,0:T(4,128)S(1)} %get-tuple-element.41), channel_id=1, source_target_pairs={{0,7},{1,6},{2,5},{3,4},{4,3},{5,2},{6,1},{7,0},{8,15},{9,14},{10,... | collective-permute-start | bytes 12296 | tf_op jit(solution)/shard_map/ppermute | solution.py:226
  26.2 0.6 %collective-permute-start.12 = (f32[128,256]{1,0:T(8,128)S(1)}, f32[128,256]{1,0:T(8,128)S(1)}, u32[]{:S(2)}, u32[]{:S(2)}) collective-permute-start(f32[128,256]{1,0:T(8,128)S(1)} %get-tuple-element.44), channel_id=1, source_target_pairs={{0,3},{1,2},{2,1},{3,0},{4,7},{5,6},{6,5},{7,4},{8,11},{9,10},{10,... | collective-permute-start | bytes 393224 | tf_op jit(solution)/shard_map/ppermute | solution.py:197
  26.7 0.4 collective-permute-done.8.refs_6_
  27.2 1.1 %collective-permute-start.13 = (f32[128,256]{1,0:T(8,128)S(1)}, f32[128,256]{1,0:T(8,128)S(1)}, u32[]{:S(2)}, u32[]{:S(2)}) collective-permute-start(f32[128,256]{1,0:T(8,128)S(1)} %get-tuple-element.45), channel_id=1, source_target_pairs={{0,4},{1,5},{2,6},{3,7},{4,0},{5,1},{6,2},{7,3},{8,12},{9,13},{10,... | collective-permute-start | bytes 393224 | tf_op jit(solution)/shard_map/ppermute | solution.py:197
  28.3 0.3 collective-permute-done.9.refs_7_
  28.6 0.6 %collective-permute-start.14 = (f32[128,256]{1,0:T(8,128)S(1)}, f32[128,256]{1,0:T(8,128)S(1)}, u32[]{:S(2)}, u32[]{:S(2)}) collective-permute-start(f32[128,256]{1,0:T(8,128)S(1)} %get-tuple-element.46), channel_id=1, source_target_pairs={{0,5},{1,4},{2,7},{3,6},{4,1},{5,0},{6,3},{7,2},{8,13},{9,12},{10,... | collective-permute-start | bytes 393224 | tf_op jit(solution)/shard_map/ppermute | solution.py:197
  29.2 1.4 %collective-permute-start.15 = (f32[128,256]{1,0:T(8,128)S(1)}, f32[128,256]{1,0:T(8,128)S(1)}, u32[]{:S(2)}, u32[]{:S(2)}) collective-permute-start(f32[128,256]{1,0:T(8,128)S(1)} %get-tuple-element.47), channel_id=1, source_target_pairs={{0,6},{1,7},{2,4},{3,5},{4,2},{5,3},{6,0},{7,1},{8,14},{9,15},{10,... | collective-permute-start | bytes 393224 | tf_op jit(solution)/shard_map/ppermute | solution.py:197
  30.6 1.3 %collective-permute-start.16 = (f32[128,256]{1,0:T(8,128)S(1)}, f32[128,256]{1,0:T(8,128)S(1)}, u32[]{:S(2)}, u32[]{:S(2)}) collective-permute-start(f32[128,256]{1,0:T(8,128)S(1)} %get-tuple-element.48), channel_id=1, source_target_pairs={{0,7},{1,6},{2,5},{3,4},{4,3},{5,2},{6,1},{7,0},{8,15},{9,14},{10,... | collective-permute-start | bytes 393224 | tf_op jit(solution)/shard_map/ppermute | solution.py:197
  31.9 4.9 %count.1 = (bf16[1024,1152]{1,0:T(8,128)(2,1)S(1)}, bf16[1024,896]{1,0:T(8,128)(2,1)S(1)}) custom-call(s32[2]{0:T(128)S(1)} %pad_add_fusion.me, s32[16,1024]{1,0:T(8,128)S(1)} %bitcast.8, s32[8,128]{1,0:T(8,128)S(1)} %bitcast.5), custom_call_target="tpu_custom_call" | custom-call | flops 1073741824 | bytes 1048576 | tf_op jit(solution)/shard_map/count/pallas_call | solution.py:232
  36.8 1.6 %near.1.base = f32[1024,256]{1,0:T(8,128)S(1)} custom-call(bf16[1024,1152]{1,0:T(8,128)(2,1)S(1)} %get-tuple-element.28.near, f32[1024,256]{1,0:T(8,128)S(1)} %copy-done.1, f32[128,256]{1,0:T(8,128)S(1)} %get-tuple-element.29.mine, s32[8,128]{1,0:T(8,128)S(1)} %bitcast.6), custom_call_target="tpu_custom_call" | custom-call | flops 1073741824 | bytes 1048576 | tf_op jit(solution)/shard_map/near/pallas_call | solution.py:245
  38.5 0.7 %collective-permute-done.13.refs_11_ = f32[128,256]{1,0:T(8,128)S(1)} collective-permute-done((f32[128,256]{1,0:T(8,128)S(1)}, f32[128,256]{1,0:T(8,128)S(1)}, u32[]{:S(2)}, u32[]{:S(2)}) %collective-permute-start.13) | collective-permute-done | bytes 131104 | tf_op jit(solution)/shard_map/ppermute | solution.py:197
  39.2 1.1 %collective-permute-done.14.refs_12_ = f32[128,256]{1,0:T(8,128)S(1)} collective-permute-done((f32[128,256]{1,0:T(8,128)S(1)}, f32[128,256]{1,0:T(8,128)S(1)}, u32[]{:S(2)}, u32[]{:S(2)}) %collective-permute-start.14) | collective-permute-done | bytes 131104 | tf_op jit(solution)/shard_map/ppermute | solution.py:197
  40.3 3.3 %last.1 = f32[1024,256]{1,0:T(8,128)} custom-call(s32[4]{0:T(128)S(1)} %copy-done.8, bf16[1024,896]{1,0:T(8,128)(2,1)S(1)} %get-tuple-element.27.adj, f32[1024,256]{1,0:T(8,128)S(1)} %near.1.base, s32[8,128]{1,0:T(8,128)S(1)} %bitcast.7, f32[256,256]{1,0:T(8,128)S(1)} %copy-done.4, f32[1,256]{1,0:T(1,128)S(1)} %bitcast.9, ...), custom_call_target="tpu_custom_call" | custom-call | flops 2147483648 | bytes 1048576 | tf_op jit(solution)/shard_map/last/pallas_call | solution.py:255
  (27 shorter events, 0.1 us)
Async XLA Ops:
  0.1 1.2 %copy-start = (f32[1024,256]{1,0:T(8,128)S(1)}, f32[1024,256]{1,0:T(8,128)}, u32[]{:S(2)}) copy-start(f32[1024,256]{1,0:T(8,128)} %features.5) | copy-start | bytes 3145732
  1.3 0.7 %copy-start.6 = (s32[8,128]{1,0:T(8,128)S(1)}, s32[8,128]{1,0:T(8,128)}, u32[]{:S(2)}) copy-start(s32[8,128]{1,0:T(8,128)} %halo.1) | copy-start | bytes 12292
  2.0 5.1 %copy-start.2 = (bf16[128,1024]{1,0:T(8,128)(2,1)S(1)}, bf16[128,1024]{1,0:T(8,128)(2,1)}, u32[]{:S(2)}) copy-start(bf16[128,1024]{1,0:T(8,128)(2,1)} %hub.3) | copy-start | bytes 786436
  2.0 29.9 %copy-start.3 = (s32[1024]{0:T(1024)S(1)}, s32[1024]{0:T(1024)}, u32[]{:S(2)}) copy-start(s32[1024]{0:T(1024)} %param.12) | copy-start | bytes 12292
  2.0 29.9 %copy-start.5 = (s32[1024,16]{0,1:T(8,128)S(1)}, s32[1024,16]{0,1:T(8,128)}, u32[]{:S(2)}) copy-start(s32[1024,16]{0,1:T(8,128)} %param.11) | copy-start | bytes 196612
  4.0 25.2 %collective-permute-start.10 = (f32[128,256]{1,0:T(8,128)S(1)}, f32[128,256]{1,0:T(8,128)S(1)}, u32[]{:S(2)}, u32[]{:S(2)}) collective-permute-start(f32[128,256]{1,0:T(8,128)S(1)} %get-tuple-element.42), channel_id=1, source_target_pairs={{0,1},{1,0},{2,3},{3,2},{4,5},{5,4},{6,7},{7,6},{8,9},{9,8},{10,11... | collective-permute-start | bytes 393224 | tf_op jit(solution)/shard_map/ppermute | solution.py:197
  4.6 26.0 %collective-permute-start.11 = (f32[128,256]{1,0:T(8,128)S(1)}, f32[128,256]{1,0:T(8,128)S(1)}, u32[]{:S(2)}, u32[]{:S(2)}) collective-permute-start(f32[128,256]{1,0:T(8,128)S(1)} %get-tuple-element.43), channel_id=1, source_target_pairs={{0,2},{1,3},{2,0},{3,1},{4,6},{5,7},{6,4},{7,5},{8,10},{9,11},{10,... | collective-permute-start | bytes 393224 | tf_op jit(solution)/shard_map/ppermute | solution.py:197
  7.9 28.9 %copy-start.1 = (f32[1024,256]{1,0:T(8,128)S(1)}, f32[1024,256]{1,0:T(8,128)}, u32[]{:S(2)}) copy-start(f32[1024,256]{1,0:T(8,128)} %features.5) | copy-start | bytes 3145732
  7.9 4.5 %collective-permute-start = (f32[32,256]{1,0:T(8,128)S(1)}, f32[32,256]{1,0:T(8,128)S(1)}, u32[]{:S(2)}, u32[]{:S(2)}) collective-permute-start(f32[32,256]{1,0:T(8,128)S(1)} %get-tuple-element.31), channel_id=1, source_target_pairs={{0,8},{8,0},{16,24},{24,16},{1,9},{9,1},{17,25},{25,17},{2,10},{10... | collective-permute-start | bytes 98312 | tf_op jit(solution)/shard_map/ppermute | solution.py:213
  9.6 5.4 %collective-permute-start.1 = (f32[32,256]{1,0:T(8,128)S(1)}, f32[32,256]{1,0:T(8,128)S(1)}, u32[]{:S(2)}, u32[]{:S(2)}) collective-permute-start(f32[32,256]{1,0:T(8,128)S(1)} %get-tuple-element.32), channel_id=1, source_target_pairs={{0,16},{8,24},{16,0},{24,8},{1,17},{9,25},{17,1},{25,9},{2,18},{10... | collective-permute-start | bytes 98312 | tf_op jit(solution)/shard_map/ppermute | solution.py:213
  12.2 5.7 %collective-permute-start.2 = (f32[32,256]{1,0:T(8,128)S(1)}, f32[32,256]{1,0:T(8,128)S(1)}, u32[]{:S(2)}, u32[]{:S(2)}) collective-permute-start(f32[32,256]{1,0:T(8,128)S(1)} %get-tuple-element.33), channel_id=1, source_target_pairs={{0,24},{8,16},{16,8},{24,0},{1,25},{9,17},{17,9},{25,1},{2,26},{10... | collective-permute-start | bytes 98312 | tf_op jit(solution)/shard_map/ppermute | solution.py:213
  18.5 1.9 %collective-permute-start.3 = (f32[4,256]{1,0:T(4,128)S(1)}, f32[4,256]{1,0:T(4,128)S(1)}, u32[]{:S(2)}, u32[]{:S(2)}) collective-permute-start(f32[4,256]{1,0:T(4,128)S(1)} %get-tuple-element.35), channel_id=1, source_target_pairs={{0,1},{1,0},{2,3},{3,2},{4,5},{5,4},{6,7},{7,6},{8,9},{9,8},{10,11... | collective-permute-start | bytes 12296 | tf_op jit(solution)/shard_map/ppermute | solution.py:226
  18.6 3.7 %collective-permute-start.4 = (f32[4,256]{1,0:T(4,128)S(1)}, f32[4,256]{1,0:T(4,128)S(1)}, u32[]{:S(2)}, u32[]{:S(2)}) collective-permute-start(f32[4,256]{1,0:T(4,128)S(1)} %get-tuple-element.36), channel_id=1, source_target_pairs={{0,2},{1,3},{2,0},{3,1},{4,6},{5,7},{6,4},{7,5},{8,10},{9,11},{10,... | collective-permute-start | bytes 12296 | tf_op jit(solution)/shard_map/ppermute | solution.py:226
  19.2 3.5 %collective-permute-start.5 = (f32[4,256]{1,0:T(4,128)S(1)}, f32[4,256]{1,0:T(4,128)S(1)}, u32[]{:S(2)}, u32[]{:S(2)}) collective-permute-start(f32[4,256]{1,0:T(4,128)S(1)} %get-tuple-element.37), channel_id=1, source_target_pairs={{0,3},{1,2},{2,1},{3,0},{4,7},{5,6},{6,5},{7,4},{8,11},{9,10},{10,... | collective-permute-start | bytes 12296 | tf_op jit(solution)/shard_map/ppermute | solution.py:226
  20.4 4.2 %collective-permute-start.6 = (f32[4,256]{1,0:T(4,128)S(1)}, f32[4,256]{1,0:T(4,128)S(1)}, u32[]{:S(2)}, u32[]{:S(2)}) collective-permute-start(f32[4,256]{1,0:T(4,128)S(1)} %get-tuple-element.38), channel_id=1, source_target_pairs={{0,4},{1,5},{2,6},{3,7},{4,0},{5,1},{6,2},{7,3},{8,12},{9,13},{10,... | collective-permute-start | bytes 12296 | tf_op jit(solution)/shard_map/ppermute | solution.py:226
  22.3 3.9 %collective-permute-start.7 = (f32[4,256]{1,0:T(4,128)S(1)}, f32[4,256]{1,0:T(4,128)S(1)}, u32[]{:S(2)}, u32[]{:S(2)}) collective-permute-start(f32[4,256]{1,0:T(4,128)S(1)} %get-tuple-element.39), channel_id=1, source_target_pairs={{0,5},{1,4},{2,7},{3,6},{4,1},{5,0},{6,3},{7,2},{8,13},{9,12},{10,... | collective-permute-start | bytes 12296 | tf_op jit(solution)/shard_map/ppermute | solution.py:226
  22.7 4.5 %collective-permute-start.8 = (f32[4,256]{1,0:T(4,128)S(1)}, f32[4,256]{1,0:T(4,128)S(1)}, u32[]{:S(2)}, u32[]{:S(2)}) collective-permute-start(f32[4,256]{1,0:T(4,128)S(1)} %get-tuple-element.40), channel_id=1, source_target_pairs={{0,6},{1,7},{2,4},{3,5},{4,2},{5,3},{6,0},{7,1},{8,14},{9,15},{10,... | collective-permute-start | bytes 12296 | tf_op jit(solution)/shard_map/ppermute | solution.py:226
  24.7 3.9 %collective-permute-start.9 = (f32[4,256]{1,0:T(4,128)S(1)}, f32[4,256]{1,0:T(4,128)S(1)}, u32[]{:S(2)}, u32[]{:S(2)}) collective-permute-start(f32[4,256]{1,0:T(4,128)S(1)} %get-tuple-element.41), channel_id=1, source_target_pairs={{0,7},{1,6},{2,5},{3,4},{4,3},{5,2},{6,1},{7,0},{8,15},{9,14},{10,... | collective-permute-start | bytes 12296 | tf_op jit(solution)/shard_map/ppermute | solution.py:226
  26.2 12.3 %collective-permute-start.12 = (f32[128,256]{1,0:T(8,128)S(1)}, f32[128,256]{1,0:T(8,128)S(1)}, u32[]{:S(2)}, u32[]{:S(2)}) collective-permute-start(f32[128,256]{1,0:T(8,128)S(1)} %get-tuple-element.44), channel_id=1, source_target_pairs={{0,3},{1,2},{2,1},{3,0},{4,7},{5,6},{6,5},{7,4},{8,11},{9,10},{10,... | collective-permute-start | bytes 393224 | tf_op jit(solution)/shard_map/ppermute | solution.py:197
  27.2 12.0 %collective-permute-start.13 = (f32[128,256]{1,0:T(8,128)S(1)}, f32[128,256]{1,0:T(8,128)S(1)}, u32[]{:S(2)}, u32[]{:S(2)}) collective-permute-start(f32[128,256]{1,0:T(8,128)S(1)} %get-tuple-element.45), channel_id=1, source_target_pairs={{0,4},{1,5},{2,6},{3,7},{4,0},{5,1},{6,2},{7,3},{8,12},{9,13},{10,... | collective-permute-start | bytes 393224 | tf_op jit(solution)/shard_map/ppermute | solution.py:197
  28.6 11.7 %collective-permute-start.14 = (f32[128,256]{1,0:T(8,128)S(1)}, f32[128,256]{1,0:T(8,128)S(1)}, u32[]{:S(2)}, u32[]{:S(2)}) collective-permute-start(f32[128,256]{1,0:T(8,128)S(1)} %get-tuple-element.46), channel_id=1, source_target_pairs={{0,5},{1,4},{2,7},{3,6},{4,1},{5,0},{6,3},{7,2},{8,13},{9,12},{10,... | collective-permute-start | bytes 393224 | tf_op jit(solution)/shard_map/ppermute | solution.py:197
  29.2 11.0 %collective-permute-start.15 = (f32[128,256]{1,0:T(8,128)S(1)}, f32[128,256]{1,0:T(8,128)S(1)}, u32[]{:S(2)}, u32[]{:S(2)}) collective-permute-start(f32[128,256]{1,0:T(8,128)S(1)} %get-tuple-element.47), channel_id=1, source_target_pairs={{0,6},{1,7},{2,4},{3,5},{4,2},{5,3},{6,0},{7,1},{8,14},{9,15},{10,... | collective-permute-start | bytes 393224 | tf_op jit(solution)/shard_map/ppermute | solution.py:197
  30.6 9.7 %collective-permute-start.16 = (f32[128,256]{1,0:T(8,128)S(1)}, f32[128,256]{1,0:T(8,128)S(1)}, u32[]{:S(2)}, u32[]{:S(2)}) collective-permute-start(f32[128,256]{1,0:T(8,128)S(1)} %get-tuple-element.48), channel_id=1, source_target_pairs={{0,7},{1,6},{2,5},{3,4},{4,3},{5,2},{6,1},{7,0},{8,15},{9,14},{10,... | collective-permute-start | bytes 393224 | tf_op jit(solution)/shard_map/ppermute | solution.py:197
  36.8 3.5 %copy-start.4 = (f32[256,256]{1,0:T(8,128)S(1)}, f32[256,256]{1,0:T(8,128)}, u32[]{:S(2)}) copy-start(f32[256,256]{1,0:T(8,128)} %weight.1) | copy-start | bytes 786436
  36.8 3.5 %copy-start.7 = (f32[256]{0:T(256)S(1)}, f32[256]{0:T(256)}, u32[]{:S(2)}) copy-start(f32[256]{0:T(256)} %param.15) | copy-start | bytes 3076
  36.8 3.5 %copy-start.8 = (s32[4]{0:T(128)S(1)}, s32[4]{0:T(128)}, u32[]{:S(2)}) copy-start(s32[4]{0:T(128)} %slot.1) | copy-start | bytes 52
